TPU v7x, 256 devices: a whole 4x4x8 slice. The times are simulated.
256 devices in a mesh: ka: 128 (over z, y, x_hi, core), ga: 2 (over x_lo).
Axes of the slice: x: 4 (x_hi: 2, x_lo: 2; x = x_hi * 2 + x_lo), y: 4, z: 8, core: 2. Of those that a mesh axis runs over, the one named last changes fastest.
Arguments:
- coeffs: bfloat16 [128, 240, 2, 64, 128], P('ka', 'ga'), may hold values from -0.44921875 to 0.44921875
- neighbour: int32 [128, 3], P('ka'), may hold values from 0 to 127, as said below
- shift_id: int32 [128, 3], P('ka'), may hold values from 0 to 7
- block_map: int32 [8, 240], replicated, may hold values from 0 to 239, as said below
Outputs:
- intersection: float32 [128, 3, 2, 64, 64], P('ka', None, None, 'ga')
Inputs may be any that keep to these rules, and one draw needn't show every extreme that they name: `neighbour`: the k-points are numbered helically. The three columns of row k hold (k + 1) mod 128, (k + 16) mod 128 and (k + 64) mod 128, in an order drawn for each row. `block_map`: each row is a permutation of the 240 blocks. Block j lies in G-slice j // 120. In every row, each G-slice receives exactly 20 of its blocks from one other G-slice, exactly 10 from each of the remaining other G-slices, and the rest from itself.
All inputs are finite; a program needn't handle non-finite values.
Results may differ from a plain program's by a relative error of at most 0.0003.
Values may be sent and summed in bfloat16 or wider, within the bound.
A program may use at most 128 MiB of HBM per device.

v0:
```python
import jax
import jax.numpy as jnp
from jax import lax
from jax.sharding import PartitionSpec as P


def shifted(block, axis, distance):
    devices = range(lax.axis_size(axis))
    route = [((i - distance) % len(devices), i) for i in devices]
    return lax.ppermute(block, axis, route)


def over_pieces(array, axis):
    return lax.all_gather(array, axis).sum(0)


def complex_intersection(bra_real, bra_imag, ket_real, ket_imag, form):
    real_part = jnp.einsum(form, bra_real, ket_real, preferred_element_type=jnp.float32)
    real_part = real_part + jnp.einsum(form, bra_imag, ket_imag, preferred_element_type=jnp.float32)
    imag_part = jnp.einsum(form, bra_real, ket_imag, preferred_element_type=jnp.float32)
    imag_part = imag_part - jnp.einsum(form, bra_imag, ket_real, preferred_element_type=jnp.float32)
    return jnp.stack([real_part, imag_part], axis=-3)


def slot_plan(
    home_slice, target_slice, sent_local, place_local, my_slice, slices, capacity, slab_blocks
):
    targets = jnp.arange(slices, dtype=jnp.int32)
    chosen = (home_slice == my_slice)[:, None, :] & (
        target_slice[:, None, :] == targets[None, :, None]
    )
    chosen = chosen & (targets != my_slice)[None, :, None]
    counted = jnp.cumsum(chosen.astype(jnp.int32), axis=2) - 1
    places = jnp.arange(capacity, dtype=jnp.int32)
    matched = (
        chosen[:, :, None, :] & (counted[:, :, None, :] == places[None, None, :, None])
    ).astype(jnp.int32)
    filled = jnp.sum(matched, axis=3)
    sent_block = jnp.sum(matched * sent_local[:, None, None, :], axis=3)
    where_to = jnp.sum(matched * place_local[:, None, None, :], axis=3) + (1 - filled) * slab_blocks
    pair_count = home_slice.shape[0]
    return (
        sent_block.reshape(pair_count, slices * capacity),
        where_to.reshape(pair_count, slices * capacity),
    )


def on_device(coeffs, neighbour, shift_id, block_map):
    k_local = coeffs.shape[0]
    slab_blocks = coeffs.shape[1]
    band_count = coeffs.shape[3]
    lane_width = coeffs.shape[4]
    vector_count = neighbour.shape[1]
    cycle_size = lax.axis_size("ka")
    slices = lax.axis_size("ga")
    my_cycle = lax.axis_index("ka")
    my_slice = lax.axis_index("ga")
    capacity = 2 * max(1, slab_blocks // 12)
    all_blocks = slab_blocks * slices
    pair_count = k_local * vector_count
    k_total = k_local * cycle_size
    row_points = min(16, k_total // 4)
    row_devices = row_points // k_local
    pad_spec = ((0, 0), (0, 1), (0, 0), (0, 0), (0, 0))
    row_point = shifted(coeffs, "ka", -1)
    row_source = jnp.mod(my_cycle + 1, cycle_size)
    plane_kets = shifted(coeffs, "ka", -row_devices)
    plane_source = jnp.mod(my_cycle + row_devices, cycle_size)
    opposite = shifted(coeffs, "ka", cycle_size // 2)
    targets_flat = neighbour.reshape(-1)
    shifts_flat = shift_id.reshape(-1)
    target_device = targets_flat // k_local
    target_lane = targets_flat - target_device * k_local
    ket_index = jnp.where(
        target_device == my_cycle,
        target_lane,
        jnp.where(
            target_device == row_source,
            k_local,
            jnp.where(
                target_device == plane_source,
                k_local + 1 + target_lane,
                2 * k_local + 1 + target_lane,
            ),
        ),
    )
    bra_index = jnp.arange(pair_count, dtype=jnp.int32) // vector_count
    picks = (
        shifts_flat[:, None] == jnp.arange(block_map.shape[0], dtype=jnp.int32)[None, :]
    ).astype(jnp.int32)
    relabel = jnp.sum(picks[:, :, None] * block_map[None, :, :], axis=1)
    dest_global = jnp.broadcast_to(jnp.arange(all_blocks, dtype=jnp.int32)[None, :], relabel.shape)
    source_slice = relabel // slab_blocks
    dest_slice = dest_global // slab_blocks
    source_local = relabel - source_slice * slab_blocks
    dest_local = dest_global - dest_slice * slab_blocks
    kets = jnp.pad(jnp.concatenate([coeffs, row_point, plane_kets, opposite], axis=0), pad_spec)
    own_source = lax.dynamic_slice_in_dim(relabel, my_slice * slab_blocks, slab_blocks, 1)
    self_place = jnp.where(
        own_source // slab_blocks == my_slice, own_source - my_slice * slab_blocks, slab_blocks
    )
    ket_self = kets[ket_index[:, None], self_place]
    ket_self = ket_self.reshape(k_local, vector_count, slab_blocks, 2, band_count, lane_width)
    local_terms = complex_intersection(
        coeffs[:, :, 0],
        coeffs[:, :, 1],
        ket_self[:, :, :, 0],
        ket_self[:, :, :, 1],
        "ksmw,kbsnw->kbmn",
    )
    sent_block, where_to = slot_plan(
        dest_slice, source_slice, dest_local, source_local, my_slice, slices, capacity, slab_blocks
    )
    payload = coeffs[bra_index[:, None], sent_block]
    owner = jnp.broadcast_to(ket_index[:, None], (pair_count, slices))
    blocks = lax.all_to_all(payload, "ga", split_axis=1, concat_axis=1, tiled=True)
    places_in = lax.all_to_all(where_to, "ga", split_axis=1, concat_axis=1, tiled=True)
    owners = lax.all_to_all(owner, "ga", split_axis=1, concat_axis=1, tiled=True)
    partner = kets[owners[:, 0][:, None], places_in]
    remote = complex_intersection(
        blocks[:, :, 0], blocks[:, :, 1], partner[:, :, 0], partner[:, :, 1], "ismw,isnw->imn"
    )
    summed_part = local_terms + remote.reshape(k_local, vector_count, 2, band_count, band_count)
    total = over_pieces(summed_part, "ga")
    row_count = band_count // slices
    return lax.dynamic_slice_in_dim(total, my_slice * row_count, row_count, 3)


def solution(mesh):
    in_specs = (P("ka", "ga", None, None, None), P("ka", None), P("ka", None), P())
    out_specs = P("ka", None, None, "ga", None)
    return jax.shard_map(
        on_device, mesh=mesh, in_specs=in_specs, out_specs=out_specs, check_vma=False
    )
```

profile of v0, /device:TPU:2, one launch (start us, length us, event | category | flops | bytes accessed | tf_op | source)
XLA Modules:
  0.0 376.7 jit_solution(13991495988785780300)
XLA Ops:
  0.0 9.3 %collective-permute-start = (bf16[1,120,2,64,128]{4,3,2,1,0:T(8,128)(2,1)}, bf16[1,120,2,64,128]{4,3,2,1,0:T(8,128)(2,1)}, u32[]{:S(2)}, u32[]{:S(2)}) collective-permute-start(bf16[1,120,2,64,128]{4,3,2,1,0:T(8,128)(2,1)} %param.4), channel_id=1, source_target_pairs={{2,0},{4,2},{6,4},{8,6},{10,8},{12,10},{14,12},{16,14},{18,16},{20... | collective-permute-start | bytes 11796488 | tf_op jit(solution)/shard_map/ppermute | solution.py:10
  9.3 1.0 collective-permute-start.1
  10.3 0.5 collective-permute-start.2
  10.9 0.7 clamp_shift-left_fusion
  11.5 0.6 broadcast_in_dim.35
  12.1 4.6 %all-to-all-start.1 = ((s32[3,2,1]{0,2,1:T(1,128)}), s32[3,2,1]{0,2,1:T(1,128)S(1)}, u32[]{:S(2)}, u32[]{:S(2)}) async-start(s32[3,2,1]{0,2,1:T(1,128)} %broadcast_in_dim.35), calls=%async_computation.1 | async-start | bytes 2048 | tf_op jit(solution)/shard_map/all_to_all | solution.py:118
  16.8 0.7 fusion.68
  17.5 0.8 multiply_reduce_fusion
  18.4 1.8 reduce-window.6
  20.3 0.1 copy.81
  20.5 0.1 copy.82
  20.6 0.1 broadcast_add_fusion
  20.7 3.1 select_reduce_fusion.1
  23.8 0.1 copy.86
  23.9 0.1 copy.87
  24.1 0.6 copy.88
  24.7 0.1 copy.83
  24.8 0.1 reshape.397
  24.9 3.3 all-to-all-start.2
  28.2 0.1 reshape.405
  28.3 5.1 %gather_fusion.1 = bf16[120,2,64,128]{3,2,1,0:T(8,128)(2,1)} fusion(bf16[1,120,2,64,128]{4,3,2,1,0:T(8,128)(2,1)} %param.4, s32[120]{0:T(128)S(1)} %reshape.405), kind=kCustom, calls=%fused_computation.1 | custom fusion | bytes 7865280 | tf_op jit(solution)/shard_map/gather | solution.py:114
  33.4 5.4 %copy.84 = bf16[3,40,2,64,128]{4,3,0,2,1:T(8,128)(2,1)} copy(bf16[3,40,2,64,128]{4,3,2,1,0:T(8,128)(2,1)} %bitcast.181) | data formatting | bytes 7864320 | tf_op jit(solution)/shard_map/gather | solution.py:114
  38.8 5.7 %all-to-all-start = ((bf16[3,40,2,64,128]{4,3,0,2,1:T(8,128)(2,1)}), bf16[3,40,2,64,128]{4,3,0,2,1:T(8,128)(2,1)}, u32[]{:S(2)}, u32[]{:S(2)}) async-start(bf16[3,40,2,64,128]{4,3,0,2,1:T(8,128)(2,1)} %copy.84), calls=%async_computation | async-start | bytes 7864320 | tf_op jit(solution)/shard_map/all_to_all | solution.py:116
  44.4 0.1 fusion.60
  44.5 0.1 reshape.399
  44.6 0.1 all_to_all.19
  44.8 0.1 reshape.411
  44.9 64.1 %all-to-all-done = bf16[3,40,2,64,128]{4,3,0,2,1:T(8,128)(2,1)} async-done(((bf16[3,40,2,64,128]{4,3,0,2,1:T(8,128)(2,1)}), bf16[3,40,2,64,128]{4,3,0,2,1:T(8,128)(2,1)}, u32[]{:S(2)}, u32[]{:S(2)}) %all-to-all-start) | async-done | bytes 3932192 | tf_op jit(solution)/shard_map/all_to_all | solution.py:116
  109.0 4.5 %fusion.77 = (bf16[3,40,1,64,128]{4,3,0,2,1:T(8,128)(2,1)S(1)}, bf16[3,40,1,64,128]{4,3,0,2,1:T(8,128)(2,1)}) fusion(bf16[3,40,2,64,128]{4,3,0,2,1:T(8,128)(2,1)} %all-to-all-done), kind=kLoop, calls=%fused_computation.110 | loop fusion | bytes 7864320 | tf_op jit(solution)/shard_map/slice | solution.py:121
  113.5 188.2 %collective-permute-done.1 = bf16[1,120,2,64,128]{4,3,2,1,0:T(8,128)(2,1)} collective-permute-done((bf16[1,120,2,64,128]{4,3,2,1,0:T(8,128)(2,1)}, bf16[1,120,2,64,128]{4,3,2,1,0:T(8,128)(2,1)}, u32[]{:S(2)}, u32[]{:S(2)}) %collective-permute-start.1) | collective-permute-done | bytes 3932192 | tf_op jit(solution)/shard_map/ppermute | solution.py:10
  301.7 12.7 %fusion.6 = bf16[4,121,2,64,128]{4,3,2,1,0:T(8,128)(2,1)} fusion(bf16[1,120,2,64,128]{4,3,2,1,0:T(8,128)(2,1)} %collective-permute-done.2, bf16[1,120,2,64,128]{4,3,2,1,0:T(8,128)(2,1)} %collective-permute-done.1, bf16[1,120,2,64,128]{4,3,2,1,0:T(8,128)(2,1)} %collective-permute-done, bf16[1,120,2,64,128]{4,3,2,1,0:T(8,128)(2,1)S(1)} %copy-done), kind=kLoop, calls=%fused_computation.10 | loop fusion | flops 103088128 | bytes 31588352 | tf_op jit(solution)/shard_map/concatenate | solution.py:97
  314.4 8.8 %gather_fusion.2 = bf16[120,2,64,128]{3,2,1,0:T(8,128)(2,1)} fusion(bf16[4,121,2,64,128]{4,3,2,1,0:T(8,128)(2,1)} %fusion.6, s32[120]{0:T(128)S(1)} %reshape.411), kind=kCustom, calls=%fused_computation.2 | custom fusion | bytes 7865280 | tf_op jit(solution)/shard_map/gather | solution.py:119
  323.3 3.1 copy.90
  326.4 0.6 fusion.23
  327.1 1.3 copy-done.2
  328.4 0.6 fusion.24
  329.0 25.5 %gather_fusion = bf16[360,2,64,128]{3,2,1,0:T(8,128)(2,1)} fusion(bf16[4,121,2,64,128]{4,3,2,1,0:T(8,128)(2,1)} %fusion.6, s32[360]{0:T(512)S(1)} %reshape.399), kind=kCustom, calls=%fused_computation | custom fusion | bytes 23595840 | tf_op jit(solution)/shard_map/gather | solution.py:102
  354.5 6.5 %copy.78 = bf16[360,2,64,128]{3,2,0,1:T(8,128)(2,1)S(1)} copy(bf16[360,2,64,128]{3,2,1,0:T(8,128)(2,1)} %gather_fusion) | data formatting | bytes 23592960 | tf_op jit(solution)/shard_map/gather | solution.py:102
  361.0 1.7 fusion.27
  362.7 1.7 fusion.36
  364.4 0.4 copy-done.3
  364.8 0.7 fusion.54
  365.5 0.7 fusion.52
  366.2 1.7 fusion.42
  367.9 1.7 fusion.48
  369.6 0.1 copy.96
  369.7 6.3 %all_gather.4 = f32[2,1,3,2,64,64]{5,4,3,2,1,0:T(8,128)S(1)} all-gather(f32[1,1,3,2,64,64]{5,4,3,2,1,0:T(8,128)S(1)} %copy.96), channel_id=1, replica_groups=mesh['ka'=128,'ga'=2] {'ga'}, dimensions={0}, use_global_device_ids=true | all-gather | bytes 294912 | tf_op jit(solution)/shard_map/all_gather | solution.py:14
  376.1 0.7 dynamic-slice_bitcast_fusion
  (33 shorter events, 0.6 us)
Async XLA Ops:
  0.0 113.5 %collective-permute-start = (bf16[1,120,2,64,128]{4,3,2,1,0:T(8,128)(2,1)}, bf16[1,120,2,64,128]{4,3,2,1,0:T(8,128)(2,1)}, u32[]{:S(2)}, u32[]{:S(2)}) collective-permute-start(bf16[1,120,2,64,128]{4,3,2,1,0:T(8,128)(2,1)} %param.4), channel_id=1, source_target_pairs={{2,0},{4,2},{6,4},{8,6},{10,8},{12,10},{14,12},{16,14},{18,16},{20... | collective-permute-start | bytes 11796488 | tf_op jit(solution)/shard_map/ppermute | solution.py:10
  9.3 292.4 %collective-permute-start.1 = (bf16[1,120,2,64,128]{4,3,2,1,0:T(8,128)(2,1)}, bf16[1,120,2,64,128]{4,3,2,1,0:T(8,128)(2,1)}, u32[]{:S(2)}, u32[]{:S(2)}) collective-permute-start(bf16[1,120,2,64,128]{4,3,2,1,0:T(8,128)(2,1)} %param.4), channel_id=1, source_target_pairs={{32,0},{34,2},{36,4},{38,6},{40,8},{42,10},{44,12},{46,14},{48,16}... | collective-permute-start | bytes 11796488 | tf_op jit(solution)/shard_map/ppermute | solution.py:10
  10.3 291.4 %collective-permute-start.2 = (bf16[1,120,2,64,128]{4,3,2,1,0:T(8,128)(2,1)}, bf16[1,120,2,64,128]{4,3,2,1,0:T(8,128)(2,1)}, u32[]{:S(2)}, u32[]{:S(2)}) collective-permute-start(bf16[1,120,2,64,128]{4,3,2,1,0:T(8,128)(2,1)} %param.4), channel_id=1, source_target_pairs={{128,0},{130,2},{132,4},{134,6},{136,8},{138,10},{140,12},{142,14}... | collective-permute-start | bytes 11796488 | tf_op jit(solution)/shard_map/ppermute | solution.py:10
  12.1 12.8 %all-to-all-start.1 = ((s32[3,2,1]{0,2,1:T(1,128)}), s32[3,2,1]{0,2,1:T(1,128)S(1)}, u32[]{:S(2)}, u32[]{:S(2)}) async-start(s32[3,2,1]{0,2,1:T(1,128)} %broadcast_in_dim.35), calls=%async_computation.1 | async-start | bytes 2048 | tf_op jit(solution)/shard_map/all_to_all | solution.py:118
  24.9 13.9 %all-to-all-start.2 = ((s32[3,2,20]{2,0,1:T(4,128)}), s32[3,2,20]{2,0,1:T(4,128)S(1)}, u32[]{:S(2)}, u32[]{:S(2)}) async-start(s32[3,2,20]{2,0,1:T(4,128)} %copy.88), calls=%async_computation.2 | async-start | bytes 8192 | tf_op jit(solution)/shard_map/all_to_all | solution.py:117
  38.8 70.2 %all-to-all-start = ((bf16[3,40,2,64,128]{4,3,0,2,1:T(8,128)(2,1)}), bf16[3,40,2,64,128]{4,3,0,2,1:T(8,128)(2,1)}, u32[]{:S(2)}, u32[]{:S(2)}) async-start(bf16[3,40,2,64,128]{4,3,0,2,1:T(8,128)(2,1)} %copy.84), calls=%async_computation | async-start | bytes 7864320 | tf_op jit(solution)/shard_map/all_to_all | solution.py:116
  109.0 192.7 %copy-start = (bf16[1,120,2,64,128]{4,3,2,1,0:T(8,128)(2,1)S(1)}, bf16[1,120,2,64,128]{4,3,2,1,0:T(8,128)(2,1)}, u32[]{:S(2)}) copy-start(bf16[1,120,2,64,128]{4,3,2,1,0:T(8,128)(2,1)} %param.4) | copy-start | bytes 11796484
  323.3 3.2 copy-start.4
  326.4 2.0 copy-start.2
  354.5 6.5 %copy-start.1 = (bf16[1,120,2,64,128]{4,3,2,1,0:T(8,128)(2,1)S(1)}, bf16[1,120,2,64,128]{4,3,2,1,0:T(8,128)(2,1)}, u32[]{:S(2)}) copy-start(bf16[1,120,2,64,128]{4,3,2,1,0:T(8,128)(2,1)} %param.4) | copy-start | bytes 11796484
  362.7 2.1 copy-start.3
where the time goes:
time: 379 us; the launch traced here: 377 us
  waiting for transfers between devices  252 us (66%)
  local copies, waits for them, and re-layouts  63.7 us (17%)
  starting transfers between devices  24.5 us (6%)
  other arithmetic  20.4 us (5%)
  matrix products  9.29 us (2%)
  blocking collectives  6.34 us (2%)
    ppermute x3, waiting for transfers between devices, shifted(): return lax.ppermute(block, axis, route)  188 us
    all_to_all x1, waiting for transfers between devices, on_device(): lax.all_to_all(payload, 'ga', split_axis=1, concat_axis=1, tiled=True)  64.1 us
    gather x2, local copies, waits for them, and re-layouts, on_device(): ket_self = kets[ket_index[:, None], self_place]  32 us
    concatenate x1, other arithmetic, on_device(): jnp.concatenate([coeffs, row_point, plane_kets, opposite], axis=0)  12.7 us
    gather x2, local copies, waits for them, and re-layouts, on_device(): partner = kets[owners[:, 0][:, None], places_in]  11.9 us
    ppermute x3, starting transfers between devices, shifted(): return lax.ppermute(block, axis, route)  10.9 us
    gather x2, local copies, waits for them, and re-layouts, on_device(): payload = coeffs[bra_index[:, None], sent_block]  10.5 us
  transfers between devices with their start and end apart: 6, of which 2 were waited for; matrix products, arithmetic and copies ran while one was open for 7% of the time, Pallas kernels for 0%

commit v1 on v0

v1 whole, which is shorter than its diff:
```python
import functools

import jax
import jax.numpy as jnp
from jax import lax
from jax.experimental import pallas as pl
from jax.experimental.pallas import tpu as pltpu
from jax.sharding import PartitionSpec as P

MESH = pl.DeviceIdType.MESH
CHUNKS = 6
STEP = 4
CONTRACT = (((1,), (1,)), ((), ()))

LOAD, ROW_SENT, RIGHT1_SENT, RIGHT1_IN, RIGHT2_SENT, RIGHT2_IN = range(6)
LEFT1_SENT, LEFT1_IN, LEFT2_SENT, LEFT2_IN, EXTRA_SENT, EXTRA_IN = range(6, 12)
RELAY_IN, RELAY_SENT, ROW_IN = range(12, 15)
ROW_JOB, NEXT_JOB, PREV_JOB, FAR_JOB, BACK_JOB = range(5)


def flipped(block):
    half = block.shape[1] // 2
    return jnp.concatenate([block[:, half:], -block[:, :half]], axis=1)


def kernel(
    n_ka, row, cross, table, coeffs, out,
    own, packed, right1, right2, left1, left2, extra, relay, ahead,
    row_out, row_in, cross_out, cross_in, parts, inbox,
    chunk_sem, row_cross_sem, cross_sem, result_sem,
):
    blocks = own.shape[0]
    bands = packed.shape[2]
    size = blocks // CHUNKS
    inside = blocks - cross
    per_job = 2 * blocks + 2 * cross
    ka = lax.axis_index("ka")
    ga = lax.axis_index("ga")
    other = 1 - ga
    core = lax.rem(ka, 2)
    plane = ka // row
    quad = lax.rem(plane, 4)
    half = plane // 4
    next_half = lax.rem(plane + 1, 8) // 4

    def at(step):
        return lax.rem(ka + n_ka + step, n_ka)

    def part(c):
        return pl.ds(c * size, size)

    def remote(source, target, sent, arrived, device):
        return pltpu.make_async_remote_copy(
            src_ref=source, dst_ref=target, send_sem=sent, recv_sem=arrived,
            device_id=device, device_id_type=MESH,
        )

    def load(c):
        return pltpu.make_async_copy(
            coeffs.at[part(c)], own.at[part(c)], chunk_sem.at[LOAD, c]
        )

    def row_direct(c):
        return remote(
            own.at[part(c)], ahead.at[part(c)],
            chunk_sem.at[ROW_SENT, c], chunk_sem.at[ROW_IN, c], (at(-1), ga),
        )

    def row_relayed(c):
        return remote(
            own.at[part(c)], relay.at[part(c)],
            chunk_sem.at[ROW_SENT, c], chunk_sem.at[RELAY_IN, c], (at(-1), other),
        )

    def relayed(c):
        return remote(
            relay.at[part(c)], ahead.at[part(c)],
            chunk_sem.at[RELAY_SENT, c], chunk_sem.at[ROW_IN, c], (ka, other),
        )

    def hop_right(c):
        return remote(
            packed.at[half, part(c)], right1.at[part(c)],
            chunk_sem.at[RIGHT1_SENT, c], chunk_sem.at[RIGHT1_IN, c], (at(row), ga),
        )

    def hop_left(c):
        return remote(
            packed.at[1 - half, part(c)], left1.at[part(c)],
            chunk_sem.at[LEFT1_SENT, c], chunk_sem.at[LEFT1_IN, c], (at(-row), ga),
        )

    def on_right(c):
        return remote(
            right1.at[part(c)], right2.at[part(c)],
            chunk_sem.at[RIGHT2_SENT, c], chunk_sem.at[RIGHT2_IN, c], (at(row), ga),
        )

    def on_left(c):
        return remote(
            left1.at[part(c)], left2.at[part(c)],
            chunk_sem.at[LEFT2_SENT, c], chunk_sem.at[LEFT2_IN, c], (at(-row), ga),
        )

    def hop_extra(c):
        return remote(
            packed.at[1 - half, part(c)], extra.at[part(c)],
            chunk_sem.at[EXTRA_SENT, c], chunk_sem.at[EXTRA_IN, c], (at(row), ga),
        )

    def swap_row():
        return remote(row_out, row_in, row_cross_sem.at[0], row_cross_sem.at[1], (ka, other))

    def swap(i):
        return remote(
            cross_out.at[i], cross_in.at[i], cross_sem.at[0, i], cross_sem.at[1, i], (ka, other)
        )

    def result(slot):
        job, step, same = RESULTS[slot]
        side = ga if same else other
        return remote(
            parts.at[job, side], inbox.at[slot],
            result_sem.at[0, slot], result_sem.at[1, slot], (at(step * row), side),
        )

    RESULTS = (
        (ROW_JOB, 0, False), (NEXT_JOB, 0, False),
        (PREV_JOB, -1, True), (PREV_JOB, -1, False),
        (FAR_JOB, -2, True), (FAR_JOB, -2, False),
        (BACK_JOB, 2, True), (BACK_JOB, 2, False),
    )

    def each(body):
        def run(c, carry):
            body(c)
            return carry
        lax.fori_loop(0, CHUNKS, run, 0)

    def bra_at(job, t):
        return table[job * per_job + t]

    def ket_at(job, t):
        return table[job * per_job + blocks + t]

    def far_ket_at(job, t):
        return table[job * per_job + 2 * blocks + cross + t]

    def gather(target, source, place):
        def run(t, carry):
            target[t] = source[place(t)]
            return carry
        lax.fori_loop(0, cross, run, 0)

    def whole_sum(total, bra, ket, count):
        def run(s, total):
            left = jnp.concatenate([bra(s * STEP + u) for u in range(STEP)], axis=1)
            right = jnp.concatenate([ket(s * STEP + u) for u in range(STEP)], axis=1)
            return total + lax.dot_general(
                left, right, CONTRACT, preferred_element_type=jnp.float32
            )
        return lax.fori_loop(0, count // STEP, run, total)

    def packed_sum(total, bra, ket, count):
        def run(s, total):
            left = jnp.concatenate([bra(s * STEP + u) for u in range(STEP)], axis=1)
            kets = [ket(s * STEP + u) for u in range(STEP)]
            right = jnp.concatenate(
                [jnp.concatenate(kets, axis=1),
                 jnp.concatenate([flipped(k) for k in kets], axis=1)], axis=0
            )
            return total + lax.dot_general(
                left, right, CONTRACT, preferred_element_type=jnp.float32
            )
        return lax.fori_loop(0, count // STEP, run, total)

    def keep(job, total):
        parts[job] = total.reshape(parts.shape[1:])

    zero = jnp.zeros((bands, 2 * bands), jnp.float32)

    each(lambda c: load(c).start())

    barrier = pltpu.get_barrier_semaphore()
    meet = [
        (ka, other), (at(row), ga), (at(-row), ga), (at(row), other), (at(-row), other),
        (at(2 * row), ga), (at(-2 * row), ga), (at(2 * row), other), (at(-2 * row), other),
        (at(-1), jnp.where(core == 1, ga, other)), (at(1), jnp.where(core == 0, ga, other)),
    ]
    for device in meet:
        pl.semaphore_signal(barrier, inc=1, device_id=device, device_id_type=MESH)
    pl.semaphore_wait(barrier, len(meet))

    def pack_chunk(c):
        def pack(t, carry):
            j = c * size + t
            real = own[j, pl.ds(0, bands), :]
            imag = own[j, pl.ds(bands, bands), :]
            cut = real.shape[1] // 2
            packed[0, j] = jnp.concatenate([real[:, :cut], imag[:, :cut]], axis=1)
            packed[1, j] = jnp.concatenate([real[:, cut:], imag[:, cut:]], axis=1)
            return carry
        lax.fori_loop(0, size, pack, 0)

    def first_sends(c):
        load(c).wait()

        @pl.when(core == 1)
        def _():
            row_direct(c).start()

        @pl.when(core == 0)
        def _():
            row_relayed(c).start()

        pack_chunk(c)

        @pl.when(c > 0)
        def _():
            hop_right(c - 1).start()
            hop_left(c - 1).start()

    each(first_sends)
    gather(row_out, own, lambda t: bra_at(ROW_JOB, inside + t))
    hop_right(CHUNKS - 1).start()
    hop_left(CHUNKS - 1).start()
    gather(cross_out.at[0], packed.at[1 - next_half], lambda t: bra_at(NEXT_JOB, inside + t))
    gather(cross_out.at[1], packed.at[half], lambda t: far_ket_at(PREV_JOB, t))
    swap_row().start()
    swap(0).start()
    swap(1).start()

    def pass_on(c):
        hop_right(c).wait_recv()
        on_right(c).start()
        hop_left(c).wait_recv()
        on_left(c).start()

        @pl.when(core == 1)
        def _():
            row_relayed(c).wait_recv()
            relayed(c).start()

    each(pass_on)

    @pl.when(quad == 3)
    def _():
        each(lambda c: hop_extra(c).start())

    swap(0).wait_recv()
    total = packed_sum(
        zero,
        lambda t: packed[1 - next_half, bra_at(NEXT_JOB, t)],
        lambda t: left1[ket_at(NEXT_JOB, t)],
        inside,
    )
    total = packed_sum(
        total, lambda t: cross_in[0, t], lambda t: left1[far_ket_at(NEXT_JOB, t)], cross
    )
    keep(NEXT_JOB, total)

    swap(1).wait_recv()

    def previous(bra):
        total = packed_sum(
            zero,
            lambda t: bra[bra_at(PREV_JOB, t)],
            lambda t: packed[half, ket_at(PREV_JOB, t)],
            inside,
        )
        total = packed_sum(
            total, lambda t: bra[bra_at(PREV_JOB, inside + t)], lambda t: cross_in[1, t], cross
        )
        keep(PREV_JOB, total)

    @pl.when(quad != 0)
    def _():
        previous(right1)

    result(1).start()

    each(lambda c: row_direct(c).wait_recv())
    swap_row().wait_recv()
    total = whole_sum(
        jnp.zeros((2 * bands, 2 * bands), jnp.float32),
        lambda t: own[bra_at(ROW_JOB, t)],
        lambda t: ahead[ket_at(ROW_JOB, t)],
        inside,
    )
    total = whole_sum(
        total, lambda t: row_in[t], lambda t: ahead[far_ket_at(ROW_JOB, t)], cross
    )
    lower = total[bands:]
    keep(
        ROW_JOB,
        total[:bands] + jnp.concatenate([lower[:, bands:], -lower[:, :bands]], axis=1),
    )

    each(lambda c: on_right(c).wait_recv())
    gather(cross_out.at[2], right2, lambda t: bra_at(FAR_JOB, inside + t))
    gather(cross_out.at[3], right2, lambda t: far_ket_at(BACK_JOB, t))
    result(0).start()
    swap(2).start()
    swap(3).start()
    each(lambda c: on_left(c).wait_recv())
    far = packed_sum(
        zero,
        lambda t: right2[bra_at(FAR_JOB, t)],
        lambda t: left2[ket_at(FAR_JOB, t)],
        inside,
    )
    back = packed_sum(
        zero,
        lambda t: left2[bra_at(BACK_JOB, t)],
        lambda t: right2[ket_at(BACK_JOB, t)],
        inside,
    )
    swap(2).wait_recv()
    far = packed_sum(
        far, lambda t: cross_in[2, t], lambda t: left2[far_ket_at(FAR_JOB, t)], cross
    )
    keep(FAR_JOB, far)
    swap(3).wait_recv()
    back = packed_sum(
        back, lambda t: left2[bra_at(BACK_JOB, inside + t)], lambda t: cross_in[3, t], cross
    )
    keep(BACK_JOB, back)

    @pl.when(quad == 0)
    def _():
        each(lambda c: hop_extra(c).wait_recv())
        previous(extra)

    for slot in (4, 5, 6, 7, 2, 3):
        result(slot).start()
    for slot in range(len(RESULTS)):
        result(slot).wait_recv()
    out[0] = parts[ROW_JOB, ga] + inbox[0]
    out[1] = (parts[NEXT_JOB, ga] + inbox[1]) + (inbox[2] + inbox[3])
    out[2] = (inbox[4] + inbox[5]) + (inbox[6] + inbox[7])

    def drain(c):
        row_direct(c).wait_send()
        hop_right(c).wait_send()
        hop_left(c).wait_send()
        on_right(c).wait_send()
        on_left(c).wait_send()

        @pl.when(core == 1)
        def _():
            relayed(c).wait_send()

        @pl.when(quad == 3)
        def _():
            hop_extra(c).wait_send()

    each(drain)
    swap_row().wait_send()
    for i in range(4):
        swap(i).wait_send()
    for slot in range(len(RESULTS)):
        result(slot).wait_send()


def job_lists(maps, my_slice, blocks, cross):
    jobs = maps.shape[0]
    source = maps.reshape(jobs, 2, blocks)
    home = jnp.arange(2, dtype=jnp.int32)[None, :, None]
    same = (source // blocks) == home
    local = lax.rem(source, blocks)
    place = jnp.arange(blocks, dtype=jnp.int32)
    before = place[None, :] < place[:, None]
    kept = jnp.sum((same[:, :, None, :] & before).astype(jnp.int32), axis=3)
    rank = jnp.where(same, kept, blocks - cross + place - kept)
    hit = rank[:, :, None, :] == place[:, None]
    bra = jnp.sum(jnp.where(hit, place, 0), axis=3)
    ket = jnp.sum(jnp.where(hit, local[:, :, None, :], 0), axis=3)
    first = my_slice == 0
    own_bra = jnp.where(first, bra[:, 0], bra[:, 1])
    own_ket = jnp.where(first, ket[:, 0], ket[:, 1])
    other_bra = jnp.where(first, bra[:, 1], bra[:, 0])[:, blocks - cross:]
    other_ket = jnp.where(first, ket[:, 1], ket[:, 0])[:, blocks - cross:]
    return jnp.concatenate([own_bra, own_ket, other_bra, other_ket], axis=1).reshape(-1)


def on_device(coeffs, neighbour, shift_id, block_map):
    _, blocks, _, bands, lanes = coeffs.shape
    n_ka = lax.axis_size("ka")
    row = n_ka // 8
    cross = 2 * max(1, blocks // 12)
    ka = lax.axis_index("ka")
    ga = lax.axis_index("ga")
    steps = jnp.array([1, row, n_ka // 2], jnp.int32)
    column = jnp.mod(ka + steps, n_ka)[:, None] == neighbour[0][None, :]
    shifts = jnp.sum(jnp.where(column, shift_id[0][None, :], 0), axis=1)

    def moved(value, step):
        return lax.ppermute(value, "ka", [(i, (i + step) % n_ka) for i in range(n_ka)])

    wanted = jnp.stack([
        shifts[0], shifts[1], moved(shifts[1], row),
        moved(shifts[2], 2 * row), moved(shifts[2], -2 * row),
    ])
    picks = wanted[:, None] == jnp.arange(block_map.shape[0], dtype=jnp.int32)[None, :]
    maps = jnp.sum(jnp.where(picks[:, :, None], block_map[None], 0), axis=1)
    table = job_lists(maps, ga, blocks, cross)

    def half_buffer(*lead):
        return pltpu.VMEM((*lead, bands, lanes), jnp.bfloat16)

    def whole_buffer(*lead):
        return pltpu.VMEM((*lead, 2 * bands, lanes), jnp.bfloat16)

    found = pl.pallas_call(
        functools.partial(kernel, n_ka, row, cross),
        out_shape=jax.ShapeDtypeStruct((3, bands // 2, 2 * bands), jnp.float32),
        in_specs=[
            pl.BlockSpec(memory_space=pltpu.SMEM),
            pl.BlockSpec(memory_space=pl.ANY),
        ],
        out_specs=pl.BlockSpec(memory_space=pltpu.VMEM),
        scratch_shapes=[
            whole_buffer(blocks),
            half_buffer(2, blocks),
            half_buffer(blocks), half_buffer(blocks),
            half_buffer(blocks), half_buffer(blocks),
            half_buffer(blocks),
            whole_buffer(blocks), whole_buffer(blocks),
            whole_buffer(cross), whole_buffer(cross),
            half_buffer(4, cross), half_buffer(4, cross),
            pltpu.VMEM((5, 2, bands // 2, 2 * bands), jnp.float32),
            pltpu.VMEM((8, bands // 2, 2 * bands), jnp.float32),
            pltpu.SemaphoreType.DMA((15, CHUNKS)),
            pltpu.SemaphoreType.DMA((2,)),
            pltpu.SemaphoreType.DMA((2, 4)),
            pltpu.SemaphoreType.DMA((2, 8)),
        ],
        compiler_params=pltpu.CompilerParams(
            collective_id=0, has_side_effects=True, vmem_limit_bytes=48 * 2**20
        ),
        name="overlaps",
    )(table, coeffs.reshape(blocks, 2 * bands, lanes))
    found = found.reshape(3, bands // 2, 2, bands).transpose(0, 2, 1, 3)
    chosen = jnp.where(
        column.T[:, :, None, None, None], found[None], jnp.zeros((), jnp.float32)
    )
    return jnp.sum(chosen, axis=1)[None]


def solution(mesh):
    in_specs = (P("ka", "ga", None, None, None), P("ka", None), P("ka", None), P())
    out_specs = P("ka", None, None, "ga", None)
    return jax.shard_map(
        on_device, mesh=mesh, in_specs=in_specs, out_specs=out_specs, check_vma=False
    )
```

time: 379 us -> 182 us (0.48)
  waiting for transfers between devices: 252 us -> 4.06 us
  Pallas kernels: 0 us -> 159 us
  local copies, waits for them, and re-layouts: 63.7 us -> 3.37 us
  starting transfers between devices: 24.5 us -> 7.32 us
  other arithmetic: 20.4 us -> 6.59 us
  matrix products: 9.29 us -> 0 us
  blocking collectives: 6.34 us -> 0 us
    ppermute x3, waiting for transfers between devices: 188 us -> 4.06 us  [moved(): lax.ppermute(value, 'ka', [(i, (i + step) % n_ka) for i in range(n_ka)])]
    pallas_call x0 -> x1, Pallas kernels: none -> 159 us  [on_device(): pl.pallas_call(functools.partial(kernel, n_ka, row, cross), out_shape=jax...]
    all_to_all x3 -> x0, waiting for transfers between devices: 64.1 us -> none  [the longest x1 64.1 us: on_device(): lax.all_to_all(payload, 'ga', split_axis=1, concat_axis=1, tiled=True)]
    gather x6 -> x0, local copies, waits for them, and re-layouts: 54.4 us -> none  [the longest x2 32 us: on_device(): ket_self = kets[ket_index[:, None], self_place]]
    all_to_all x3 -> x0, starting transfers between devices: 13.6 us -> none  [the longest x1 5.67 us: on_device(): lax.all_to_all(payload, 'ga', split_axis=1, concat_axis=1, tiled=True)]
    concatenate x6 -> x1, other arithmetic: 13.6 us -> 0.08 us  [job_lists(): jnp.concatenate([own_bra, own_ket, other_bra, other_ket], axis=1)]
    dot_general x8 -> x0, matrix products: 9.29 us -> none  [the longest x2 2.37 us: complex_intersection(): jnp.einsum(form, bra_real, ket_real, preferred_element_type=jnp.float32)]
    all_gather x1 -> x0, blocking collectives: 6.34 us -> none  [over_pieces(): return lax.all_gather(array, axis).sum(0)]
  transfers between devices with their start and end apart: 6 -> 3, of which waited for: 2 -> 2; matrix products, arithmetic and copies ran while one was open for 7% -> 0% of each run, Pallas kernels for 0% -> 0%
where the time goes in v1:
time: 182 us; the launch traced here: 180 us
  Pallas kernels  159 us (87%)
  starting transfers between devices  7.32 us (4%)
  other arithmetic  6.59 us (4%)
  waiting for transfers between devices  4.06 us (2%)
  local copies, waits for them, and re-layouts  3.37 us (2%)
    pallas_call x1, Pallas kernels, on_device(): pl.pallas_call(functools.partial(kernel, n_ka, row, cross), out_shape=jax...  159 us
    ppermute x3, starting transfers between devices, moved(): lax.ppermute(value, 'ka', [(i, (i + step) % n_ka) for i in range(n_ka)])  7.32 us
    ppermute x3, waiting for transfers between devices, moved(): lax.ppermute(value, 'ka', [(i, (i + step) % n_ka) for i in range(n_ka)])  4.06 us
  transfers between devices with their start and end apart: 3, of which 2 were waited for; matrix products, arithmetic and copies ran while one was open for 0% of the time, Pallas kernels for 0%

profile of v1, /device:TPU:2, one launch (start us, length us, event | category | flops | bytes accessed | tf_op | source)
XLA Modules:
  0.0 180.4 jit_solution(7689620710635570120)
XLA Ops:
  0.0 0.7 and_select_fusion.1
  0.7 0.9 select_reduce_fusion.4
  1.5 0.7 fusion.5
  2.2 6.3 %collective-permute-start.2 = (s32[]{:T(128)}, s32[]{:T(128)}, u32[]{:S(2)}, u32[]{:S(2)}) collective-permute-start(s32[]{:T(128)} %bitcast.4), channel_id=1, source_target_pairs={{0,192},{2,194},{4,196},{6,198},{8,200},{10,202},{12,204},{14,206}... | collective-permute-start | bytes 20 | tf_op jit(solution)/shard_map/ppermute | solution.py:398
  8.5 0.0 collective-permute-start.1
  8.5 1.0 collective-permute-start
  9.5 0.7 broadcast_compare_fusion
  10.3 3.5 %collective-permute-done = s32[]{:T(128)} collective-permute-done((s32[]{:T(128)}, s32[]{:T(128)}, u32[]{:S(2)}, u32[]{:S(2)}) %collective-permute-start) | collective-permute-done | bytes 36 | tf_op jit(solution)/shard_map/ppermute | solution.py:398
  13.8 0.0 collective-permute-done.2
  13.8 0.5 collective-permute-done.1
  14.3 1.9 %pad_add_fusion.1 = s32[5]{0:T(128)S(1)} fusion(s32[1]{0:T(128)} %bitcast.6, s32[1]{0:T(128)} %bitcast.5, s32[1]{0:T(128)} %bitcast.3, s32[2]{0:T(128)S(1)} %bitcast.25), kind=kLoop, calls=%fused_computation.29 | loop fusion | flops 15 | bytes 40 | tf_op jit(solution)/shard_map/stack | solution.py:400
  16.2 0.1 iota_compare_fusion.2
  16.3 0.8 select_reduce_fusion.3
  17.1 0.1 ne.44
  17.2 0.1 rem.53
  17.3 0.1 div.17
  17.4 0.3 convert_reduce_fusion
  17.7 0.4 select_reduce_fusion.1
  18.1 0.1 slice.41
  18.2 0.1 slice.42
  18.3 0.1 pad_add_fusion
  18.4 0.1 reshape.129.table
  18.5 0.0 copy-start
  18.5 2.1 %copy-done = bf16[1,120,2,64,128]{4,3,2,1,0:T(8,128)(2,1)S(1)} copy-done((bf16[1,120,2,64,128]{4,3,2,1,0:T(8,128)(2,1)S(1)}, bf16[1,120,2,64,128]{4,3,2,1,0:T(8,128)(2,1)}, u32[]{:S(2)}) %copy-start) | copy-done | bytes 3932184
  20.6 158.9 %overlaps.1 = f32[3,32,128]{2,1,0:T(8,128)S(1)} custom-call(s32[1400]{0:T(1024)S(1)} %reshape.129.table, bf16[120,128,128]{2,1,0:T(8,128)(2,1)S(1)} %bitcast.21), custom_call_target="tpu_custom_call" | custom-call | tf_op jit(solution)/shard_map/overlaps/pallas_call | solution.py:414
  179.5 0.1 reshape.131
  179.6 0.7 select_reduce_fusion.2
  (11 shorter events, 0.1 us)
Async XLA Ops:
  2.2 11.6 %collective-permute-start.2 = (s32[]{:T(128)}, s32[]{:T(128)}, u32[]{:S(2)}, u32[]{:S(2)}) collective-permute-start(s32[]{:T(128)} %bitcast.4), channel_id=1, source_target_pairs={{0,192},{2,194},{4,196},{6,198},{8,200},{10,202},{12,204},{14,206}... | collective-permute-start | bytes 20 | tf_op jit(solution)/shard_map/ppermute | solution.py:398
  8.5 5.8 %collective-permute-start.1 = (s32[]{:T(128)}, s32[]{:T(128)}, u32[]{:S(2)}, u32[]{:S(2)}) collective-permute-start(s32[]{:T(128)} %bitcast.4), channel_id=1, source_target_pairs={{0,64},{2,66},{4,68},{6,70},{8,72},{10,74},{12,76},{14,78},{16,80}... | collective-permute-start | bytes 20 | tf_op jit(solution)/shard_map/ppermute | solution.py:398
  8.5 5.3 %collective-permute-start = (s32[]{:T(128)}, s32[]{:T(128)}, u32[]{:S(2)}, u32[]{:S(2)}) collective-permute-start(s32[]{:T(128)} %bitcast.2), channel_id=1, source_target_pairs={{0,32},{2,34},{4,36},{6,38},{8,40},{10,42},{12,44},{14,46},{16,48}... | collective-permute-start | bytes 20 | tf_op jit(solution)/shard_map/ppermute | solution.py:398
  18.5 2.1 %copy-start = (bf16[1,120,2,64,128]{4,3,2,1,0:T(8,128)(2,1)S(1)}, bf16[1,120,2,64,128]{4,3,2,1,0:T(8,128)(2,1)}, u32[]{:S(2)}) copy-start(bf16[1,120,2,64,128]{4,3,2,1,0:T(8,128)(2,1)} %param.5) | copy-start | bytes 11796484

commit v2 on v1

--- a/solution.py
+++ b/solution.py
@@ -8,14 +8,17 @@
 from jax.sharding import PartitionSpec as P
 
 MESH = pl.DeviceIdType.MESH
-CHUNKS = 6
-STEP = 4
+CHUNKS = 8
+PATHS = 4
+PACK = 5
+STEP = 20
 CONTRACT = (((1,), (1,)), ((), ()))
 
 LOAD, ROW_SENT, RIGHT1_SENT, RIGHT1_IN, RIGHT2_SENT, RIGHT2_IN = range(6)
-LEFT1_SENT, LEFT1_IN, LEFT2_SENT, LEFT2_IN, EXTRA_SENT, EXTRA_IN = range(6, 12)
-RELAY_IN, RELAY_SENT, ROW_IN = range(12, 15)
+LEFT1_SENT, LEFT1_IN, LEFT2_SENT, LEFT2_IN = range(6, 10)
+RELAY_IN, RELAY_SENT, ROW_IN = range(10, 13)
 ROW_JOB, NEXT_JOB, PREV_JOB, FAR_JOB, BACK_JOB = range(5)
+JOBS = 5
 
 
 def flipped(block):
@@ -24,24 +27,26 @@
 
 
 def kernel(
-    n_ka, row, cross, table, coeffs, out,
-    own, packed, right1, right2, left1, left2, extra, relay, ahead,
+    n_ka, row, cross, neighbour, shift_id, block_map, coeffs, out,
+    shifts_out, shifts_in, table_rows, table, own, packed, right1, right2, left1, left2, extra, extra_out, relay, via, ahead,
     row_out, row_in, cross_out, cross_in, parts, inbox,
-    chunk_sem, row_cross_sem, cross_sem, result_sem,
+    chunk_sem, shift_sem, table_sem, via_sem, extra_sem, row_cross_sem, cross_sem, result_sem,
 ):
     blocks = own.shape[0]
     bands = packed.shape[2]
+    lanes = packed.shape[3]
     size = blocks // CHUNKS
     inside = blocks - cross
-    per_job = 2 * blocks + 2 * cross
     ka = lax.axis_index("ka")
     ga = lax.axis_index("ga")
     other = 1 - ga
     core = lax.rem(ka, 2)
-    plane = ka // row
+    place = lax.rem(ka, row)
+    plane = lax.rem(ka // row + 2 * core, 8)
     quad = lax.rem(plane, 4)
     half = plane // 4
     next_half = lax.rem(plane + 1, 8) // 4
+    share = blocks // 2
 
     def at(step):
         return lax.rem(ka + n_ka + step, n_ka)
@@ -102,11 +107,26 @@
             chunk_sem.at[LEFT2_SENT, c], chunk_sem.at[LEFT2_IN, c], (at(-row), ga),
         )
 
-    def hop_extra(c):
-        return remote(
-            packed.at[1 - half, part(c)], extra.at[part(c)],
-            chunk_sem.at[EXTRA_SENT, c], chunk_sem.at[EXTRA_IN, c], (at(row), ga),
-        )
+    def hop_extra(step):
+        return remote(
+            extra_out, extra, extra_sem.at[0], extra_sem.at[1], (at(step * row), ga)
+        )
+
+    def to_via(c, p):
+        slot = c // PATHS
+        return remote(
+            own.at[part(c)], via.at[slot],
+            chunk_sem.at[ROW_SENT, c], via_sem.at[0, slot], (at(VIAS[p]), other),
+        )
+
+    def from_via(slot, p):
+        c = slot * PATHS + p
+        return remote(
+            via.at[slot], ahead.at[part(c)],
+            via_sem.at[1, slot], chunk_sem.at[ROW_IN, c], (at(-1 - VIAS[p]), other),
+        )
+
+    VIAS = {1: 2, 2: row - 4, 3: row - 2}
 
     def swap_row():
         return remote(row_out, row_in, row_cross_sem.at[0], row_cross_sem.at[1], (ka, other))
@@ -138,19 +158,20 @@
         lax.fori_loop(0, CHUNKS, run, 0)
 
     def bra_at(job, t):
-        return table[job * per_job + t]
+        return table[job, t]
 
     def ket_at(job, t):
-        return table[job * per_job + blocks + t]
+        return table[JOBS + job, t]
 
     def far_ket_at(job, t):
-        return table[job * per_job + 2 * blocks + cross + t]
-
-    def gather(target, source, place):
+        return table[2 * JOBS + job, inside + t]
+
+    def gather(target, source, spot, count=cross):
         def run(t, carry):
-            target[t] = source[place(t)]
+            for u in range(PACK):
+                target[t * PACK + u] = source[spot(t * PACK + u)]
             return carry
-        lax.fori_loop(0, cross, run, 0)
+        lax.fori_loop(0, count // PACK, run, 0)
 
     def whole_sum(total, bra, ket, count):
         def run(s, total):
@@ -181,26 +202,94 @@
 
     each(lambda c: load(c).start())
 
+    tile = (8, lanes)
+    columns = neighbour.shape[1]
+    targets = [jnp.broadcast_to(neighbour[:, b : b + 1], tile) for b in range(columns)]
+    steps = (1, row, n_ka // 2)
+
+    def shift_of(step):
+        found = jnp.zeros(tile, jnp.int32)
+        for b in range(columns):
+            moved = jnp.broadcast_to(shift_id[:, b : b + 1], tile)
+            found = found + jnp.where(targets[b] == at(step), moved, 0)
+        return found
+
+    row_shift, next_shift, far_shift = [shift_of(step) for step in steps]
+    shifts_out[0] = next_shift
+    shifts_out[1] = far_shift
+
+    def send_shift(i):
+        return remote(
+            shifts_out.at[min(i, 1)], shifts_in.at[i],
+            shift_sem.at[0, i], shift_sem.at[1, i], (at((row, 2 * row, -2 * row)[i]), ga),
+        )
+
     barrier = pltpu.get_barrier_semaphore()
     meet = [
         (ka, other), (at(row), ga), (at(-row), ga), (at(row), other), (at(-row), other),
         (at(2 * row), ga), (at(-2 * row), ga), (at(2 * row), other), (at(-2 * row), other),
         (at(-1), jnp.where(core == 1, ga, other)), (at(1), jnp.where(core == 0, ga, other)),
     ]
+    for step in VIAS.values():
+        meet += [(at(move), other) for move in (step, -step, 1 + step, -1 - step)]
     for device in meet:
         pl.semaphore_signal(barrier, inc=1, device_id=device, device_id_type=MESH)
     pl.semaphore_wait(barrier, len(meet))
+    for i in range(3):
+        send_shift(i).start()
 
     def pack_chunk(c):
         def pack(t, carry):
-            j = c * size + t
-            real = own[j, pl.ds(0, bands), :]
-            imag = own[j, pl.ds(bands, bands), :]
-            cut = real.shape[1] // 2
-            packed[0, j] = jnp.concatenate([real[:, :cut], imag[:, :cut]], axis=1)
-            packed[1, j] = jnp.concatenate([real[:, cut:], imag[:, cut:]], axis=1)
+            for u in range(PACK):
+                j = c * size + t * PACK + u
+                real = own[j, pl.ds(0, bands), :]
+                imag = own[j, pl.ds(bands, bands), :]
+                cut = real.shape[1] // 2
+                packed[0, j] = jnp.concatenate([real[:, :cut], imag[:, :cut]], axis=1)
+                packed[1, j] = jnp.concatenate([real[:, cut:], imag[:, cut:]], axis=1)
             return carry
-        lax.fori_loop(0, size, pack, 0)
+        lax.fori_loop(0, size // PACK, pack, 0)
+
+    def make_table():
+        lane = lax.broadcasted_iota(jnp.int32, (lanes, lanes), 1)
+        line = lax.broadcasted_iota(jnp.int32, (lanes, lanes), 0)
+        maps = [
+            jnp.concatenate(
+                [block_map[:, a * blocks : (a + 1) * blocks],
+                 jnp.zeros((block_map.shape[0], lanes - blocks), jnp.int32)], axis=1
+            )
+            for a in range(2)
+        ]
+        maps = [jnp.where(ga == a, maps[0], maps[1]) for a in range(2)]
+        shifts = [row_shift, next_shift] + [shifts_in[i] for i in range(3)]
+        choice = lax.broadcasted_iota(jnp.int32, tile, 0)
+        rows = [
+            jnp.sum(jnp.where(shift == choice, each_map, 0), axis=0, keepdims=True)
+            for each_map in maps for shift in shifts
+        ]
+        rows = jnp.concatenate(rows + [jnp.zeros((16 - 2 * JOBS, lanes), jnp.int32)], axis=0)
+        number = lax.broadcasted_iota(jnp.int32, rows.shape, 0)
+        spot = lax.broadcasted_iota(jnp.int32, rows.shape, 1)
+        source = jnp.where(rows >= blocks, 1, 0)
+        same = jnp.where(source == jnp.where(number < JOBS, ga, other), 1, 0)
+        local = rows - blocks * source
+        same_t = same.T
+        kept = [
+            jnp.sum(jnp.where(line < lane, same_t[:, r : r + 1], 0), axis=0, keepdims=True)
+            for r in range(2 * JOBS)
+        ]
+        kept = jnp.concatenate(kept + [jnp.zeros((16 - 2 * JOBS, lanes), jnp.int32)], axis=0)
+        rank = jnp.where(same == 1, kept, inside + spot - kept)
+        rank_t = jnp.where(spot < blocks, rank, -1).T
+        local_t = local.T
+        hits = [rank_t[:, r : r + 1] == lane for r in range(2 * JOBS)]
+        lists = [jnp.sum(jnp.where(hits[r], line, 0), axis=0, keepdims=True) for r in range(JOBS)]
+        lists += [
+            jnp.sum(jnp.where(hits[r], local_t[:, r : r + 1], 0), axis=0, keepdims=True)
+            for r in range(2 * JOBS)
+        ]
+        lists += [jnp.zeros((1, lanes), jnp.int32)]
+        table_rows[...] = jnp.concatenate(lists, axis=0)
 
     def first_sends(c):
         load(c).wait()
@@ -209,9 +298,16 @@
         def _():
             row_direct(c).start()
 
-        @pl.when(core == 0)
+        path = jnp.where(place == 0, lax.rem(c, PATHS), 0)
+
+        @pl.when((core == 0) & (path == 0))
         def _():
             row_relayed(c).start()
+
+        for p in VIAS:
+            @pl.when((core == 0) & (path == p))
+            def _(p=p):
+                to_via(c, p).start()
 
         pack_chunk(c)
 
@@ -221,9 +317,15 @@
             hop_left(c - 1).start()
 
     each(first_sends)
-    gather(row_out, own, lambda t: bra_at(ROW_JOB, inside + t))
+    for i in range(3):
+        send_shift(i).wait_recv()
+    make_table()
     hop_right(CHUNKS - 1).start()
     hop_left(CHUNKS - 1).start()
+    fetch = pltpu.make_async_copy(table_rows, table, table_sem)
+    fetch.start()
+    fetch.wait()
+    gather(row_out, own, lambda t: bra_at(ROW_JOB, inside + t))
     gather(cross_out.at[0], packed.at[1 - next_half], lambda t: bra_at(NEXT_JOB, inside + t))
     gather(cross_out.at[1], packed.at[half], lambda t: far_ket_at(PREV_JOB, t))
     swap_row().start()
@@ -236,16 +338,39 @@
         hop_left(c).wait_recv()
         on_left(c).start()
 
-        @pl.when(core == 1)
+        @pl.when((core == 1) & (place != row - 1))
         def _():
-            row_relayed(c).wait_recv()
-            relayed(c).start()
+            relay_on(c)
+
+        for p, step in VIAS.items():
+            @pl.when((place == step) & ((c == 3) | (c == 5)))
+            def _(p=p):
+                slot = (c - 3) // 2
+                to_via(slot * PATHS, p).wait_recv()
+                from_via(slot, p).start()
+
+    def relay_on(c):
+        row_relayed(c).wait_recv()
+        relayed(c).start()
 
     each(pass_on)
 
     @pl.when(quad == 3)
     def _():
-        each(lambda c: hop_extra(c).start())
+        gather(
+            extra_out, packed.at[1 - half], lambda t: bra_at(NEXT_JOB, share + t), blocks - share
+        )
+        hop_extra(1).start()
+
+    @pl.when(quad == 0)
+    def _():
+        gather(extra_out, packed.at[half], lambda t: ket_at(PREV_JOB, t), share)
+        hop_extra(-1).start()
+
+    @pl.when(place == row - 1)
+    def _():
+        for c in range(0, CHUNKS, PATHS):
+            relay_on(c)
 
     swap(0).wait_recv()
     total = packed_sum(
@@ -261,23 +386,22 @@
 
     swap(1).wait_recv()
 
-    def previous(bra):
+    @pl.when(quad != 0)
+    def _():
         total = packed_sum(
             zero,
-            lambda t: bra[bra_at(PREV_JOB, t)],
+            lambda t: right1[bra_at(PREV_JOB, t)],
             lambda t: packed[half, ket_at(PREV_JOB, t)],
             inside,
         )
         total = packed_sum(
-            total, lambda t: bra[bra_at(PREV_JOB, inside + t)], lambda t: cross_in[1, t], cross
+            total, lambda t: right1[bra_at(PREV_JOB, inside + t)], lambda t: cross_in[1, t], cross
         )
         keep(PREV_JOB, total)
 
-    @pl.when(quad != 0)
-    def _():
-        previous(right1)
-
-    result(1).start()
+    @pl.when(quad != 3)
+    def _():
+        result(1).start()
 
     each(lambda c: row_direct(c).wait_recv())
     swap_row().wait_recv()
@@ -300,6 +424,12 @@
     gather(cross_out.at[2], right2, lambda t: bra_at(FAR_JOB, inside + t))
     gather(cross_out.at[3], right2, lambda t: far_ket_at(BACK_JOB, t))
     result(0).start()
+
+    @pl.when(quad != 0)
+    def _():
+        result(2).start()
+        result(3).start()
+
     swap(2).start()
     swap(3).start()
     each(lambda c: on_left(c).wait_recv())
@@ -326,18 +456,50 @@
     )
     keep(BACK_JOB, back)
 
+    for slot in (4, 5, 6, 7):
+        result(slot).start()
+
+    @pl.when(quad == 3)
+    def _():
+        hop_extra(1).wait_recv()
+        more = packed_sum(
+            zero,
+            lambda t: packed[1 - half, bra_at(NEXT_JOB, t)],
+            lambda t: extra[t],
+            share,
+        )
+        keep(NEXT_JOB, parts[NEXT_JOB].reshape(zero.shape) + more)
+        result(1).start()
+
     @pl.when(quad == 0)
     def _():
-        each(lambda c: hop_extra(c).wait_recv())
-        previous(extra)
-
-    for slot in (4, 5, 6, 7, 2, 3):
-        result(slot).start()
+        hop_extra(-1).wait_recv()
+        total = packed_sum(
+            zero,
+            lambda t: extra[t],
+            lambda t: packed[half, ket_at(PREV_JOB, share + t)],
+            inside - share,
+        )
+        total = packed_sum(
+            total, lambda t: extra[inside - share + t], lambda t: cross_in[1, t], cross
+        )
+        keep(PREV_JOB, total)
+        result(2).start()
+        result(3).start()
     for slot in range(len(RESULTS)):
         result(slot).wait_recv()
-    out[0] = parts[ROW_JOB, ga] + inbox[0]
-    out[1] = (parts[NEXT_JOB, ga] + inbox[1]) + (inbox[2] + inbox[3])
-    out[2] = (inbox[4] + inbox[5]) + (inbox[6] + inbox[7])
+    found = [
+        parts[ROW_JOB, ga] + inbox[0],
+        (parts[NEXT_JOB, ga] + inbox[1]) + (inbox[2] + inbox[3]),
+        (inbox[4] + inbox[5]) + (inbox[6] + inbox[7]),
+    ]
+    for b in range(columns):
+        target = jnp.broadcast_to(neighbour[:, b : b + 1], found[0].shape)
+        chosen = jnp.where(
+            target == at(steps[0]), found[0], jnp.where(target == at(steps[1]), found[1], found[2])
+        )
+        out[b, 0] = chosen[:, :bands]
+        out[b, 1] = chosen[:, bands:]
 
     def drain(c):
         row_direct(c).wait_send()
@@ -346,15 +508,24 @@
         on_right(c).wait_send()
         on_left(c).wait_send()
 
-        @pl.when(core == 1)
+        @pl.when((core == 1) & ((place != row - 1) | (lax.rem(c, PATHS) == 0)))
         def _():
             relayed(c).wait_send()
 
-        @pl.when(quad == 3)
-        def _():
-            hop_extra(c).wait_send()
-
     each(drain)
+    for i in range(3):
+        send_shift(i).wait_send()
+
+    @pl.when((quad == 3) | (quad == 0))
+    def _():
+        hop_extra(1).wait_send()
+
+    for p, step in VIAS.items():
+        @pl.when(place == step)
+        def _(p=p):
+            for slot in range(CHUNKS // PATHS):
+                from_via(slot, p).wait_send()
+
     swap_row().wait_send()
     for i in range(4):
         swap(i).wait_send()
@@ -362,49 +533,12 @@
         result(slot).wait_send()
 
 
-def job_lists(maps, my_slice, blocks, cross):
-    jobs = maps.shape[0]
-    source = maps.reshape(jobs, 2, blocks)
-    home = jnp.arange(2, dtype=jnp.int32)[None, :, None]
-    same = (source // blocks) == home
-    local = lax.rem(source, blocks)
-    place = jnp.arange(blocks, dtype=jnp.int32)
-    before = place[None, :] < place[:, None]
-    kept = jnp.sum((same[:, :, None, :] & before).astype(jnp.int32), axis=3)
-    rank = jnp.where(same, kept, blocks - cross + place - kept)
-    hit = rank[:, :, None, :] == place[:, None]
-    bra = jnp.sum(jnp.where(hit, place, 0), axis=3)
-    ket = jnp.sum(jnp.where(hit, local[:, :, None, :], 0), axis=3)
-    first = my_slice == 0
-    own_bra = jnp.where(first, bra[:, 0], bra[:, 1])
-    own_ket = jnp.where(first, ket[:, 0], ket[:, 1])
-    other_bra = jnp.where(first, bra[:, 1], bra[:, 0])[:, blocks - cross:]
-    other_ket = jnp.where(first, ket[:, 1], ket[:, 0])[:, blocks - cross:]
-    return jnp.concatenate([own_bra, own_ket, other_bra, other_ket], axis=1).reshape(-1)
-
-
 def on_device(coeffs, neighbour, shift_id, block_map):
     _, blocks, _, bands, lanes = coeffs.shape
+    columns = neighbour.shape[1]
     n_ka = lax.axis_size("ka")
     row = n_ka // 8
     cross = 2 * max(1, blocks // 12)
-    ka = lax.axis_index("ka")
-    ga = lax.axis_index("ga")
-    steps = jnp.array([1, row, n_ka // 2], jnp.int32)
-    column = jnp.mod(ka + steps, n_ka)[:, None] == neighbour[0][None, :]
-    shifts = jnp.sum(jnp.where(column, shift_id[0][None, :], 0), axis=1)
-
-    def moved(value, step):
-        return lax.ppermute(value, "ka", [(i, (i + step) % n_ka) for i in range(n_ka)])
-
-    wanted = jnp.stack([
-        shifts[0], shifts[1], moved(shifts[1], row),
-        moved(shifts[2], 2 * row), moved(shifts[2], -2 * row),
-    ])
-    picks = wanted[:, None] == jnp.arange(block_map.shape[0], dtype=jnp.int32)[None, :]
-    maps = jnp.sum(jnp.where(picks[:, :, None], block_map[None], 0), axis=1)
-    table = job_lists(maps, ga, blocks, cross)
-
     def half_buffer(*lead):
         return pltpu.VMEM((*lead, bands, lanes), jnp.bfloat16)
 
@@ -413,38 +547,45 @@
 
     found = pl.pallas_call(
         functools.partial(kernel, n_ka, row, cross),
-        out_shape=jax.ShapeDtypeStruct((3, bands // 2, 2 * bands), jnp.float32),
+        out_shape=jax.ShapeDtypeStruct((columns, 2, bands // 2, bands), jnp.float32),
         in_specs=[
-            pl.BlockSpec(memory_space=pltpu.SMEM),
+            pl.BlockSpec(memory_space=pltpu.VMEM),
+            pl.BlockSpec(memory_space=pltpu.VMEM),
+            pl.BlockSpec(memory_space=pltpu.VMEM),
             pl.BlockSpec(memory_space=pl.ANY),
         ],
         out_specs=pl.BlockSpec(memory_space=pltpu.VMEM),
         scratch_shapes=[
+            pltpu.VMEM((2, 8, lanes), jnp.int32),
+            pltpu.VMEM((3, 8, lanes), jnp.int32),
+            pltpu.VMEM((16, lanes), jnp.int32),
+            pltpu.SMEM((16, lanes), jnp.int32),
             whole_buffer(blocks),
             half_buffer(2, blocks),
             half_buffer(blocks), half_buffer(blocks),
             half_buffer(blocks), half_buffer(blocks),
-            half_buffer(blocks),
-            whole_buffer(blocks), whole_buffer(blocks),
+            half_buffer(blocks // 2), half_buffer(blocks // 2),
+            whole_buffer(blocks), whole_buffer(CHUNKS // PATHS, blocks // CHUNKS),
+            whole_buffer(blocks),
             whole_buffer(cross), whole_buffer(cross),
             half_buffer(4, cross), half_buffer(4, cross),
             pltpu.VMEM((5, 2, bands // 2, 2 * bands), jnp.float32),
             pltpu.VMEM((8, bands // 2, 2 * bands), jnp.float32),
-            pltpu.SemaphoreType.DMA((15, CHUNKS)),
+            pltpu.SemaphoreType.DMA((13, CHUNKS)),
+            pltpu.SemaphoreType.DMA((2, 3)),
+            pltpu.SemaphoreType.DMA,
+            pltpu.SemaphoreType.DMA((2, CHUNKS // PATHS)),
+            pltpu.SemaphoreType.DMA((2,)),
             pltpu.SemaphoreType.DMA((2,)),
             pltpu.SemaphoreType.DMA((2, 4)),
             pltpu.SemaphoreType.DMA((2, 8)),
         ],
         compiler_params=pltpu.CompilerParams(
-            collective_id=0, has_side_effects=True, vmem_limit_bytes=48 * 2**20
+            collective_id=0, has_side_effects=True, vmem_limit_bytes=61 * 2**20
         ),
         name="overlaps",
-    )(table, coeffs.reshape(blocks, 2 * bands, lanes))
-    found = found.reshape(3, bands // 2, 2, bands).transpose(0, 2, 1, 3)
-    chosen = jnp.where(
-        column.T[:, :, None, None, None], found[None], jnp.zeros((), jnp.float32)
-    )
-    return jnp.sum(chosen, axis=1)[None]
+    )(neighbour, shift_id, block_map, coeffs.reshape(blocks, 2 * bands, lanes))
+    return found[None]
 
 
 def solution(mesh):

time: 182 us -> 130 us (0.71)
  the two profiles are of different devices: /device:TPU:2 before, /device:TPU:98 now
where the time goes in v2:
time: 130 us; the launch traced here: 129 us
  Pallas kernels  128 us (98%)
  local copies, waits for them, and re-layouts  1.54 us (1%)
    pallas_call x1, Pallas kernels, on_device(): pl.pallas_call(functools.partial(kernel, n_ka, row, cross), out_shape=jax...  128 us

profile of v2, /device:TPU:98, one launch (start us, length us, event | category | flops | bytes accessed | tf_op | source)
XLA Modules:
  0.0 129.4 jit_solution(4077882778524318485)
XLA Ops:
  0.0 127.9 %overlaps.1 = f32[3,2,32,64]{3,2,1,0:T(8,128)} custom-call(s32[1,3]{1,0:T(1,128)} %neighbour.1, s32[1,3]{1,0:T(1,128)} %shift_id.1, s32[8,240]{1,0:T(8,128)} %block_map.1, bf16[120,128,128]{2,1,0:T(8,128)(2,1)} %bitcast.2), custom_call_target="tpu_custom_call" | custom-call | tf_op jit(solution)/shard_map/overlaps/pallas_call | solution.py:548
  127.9 1.5 %copy.6 = f32[1,3,2,32,64]{4,3,2,1,0:T(8,128)} copy(f32[1,3,2,32,64]{4,3,2,1,0:T(8,128)} %bitcast.3) | data formatting | bytes 98304

commit v3 on v2

v3 whole, which is shorter than its diff:
```python
import functools

import jax
import jax.numpy as jnp
from jax import lax
from jax.experimental import pallas as pl
from jax.experimental.pallas import tpu as pltpu
from jax.sharding import PartitionSpec as P

MESH = pl.DeviceIdType.MESH
CHUNKS = 8
CUTS = 4
TURNS = 6
LEFT_OWN, LEFT_BESIDE = (0,), (1,)
RIGHT_OWN, RIGHT_BESIDE = (2, 3), (4, 5)
LEFT = LEFT_OWN + LEFT_BESIDE
RIGHT = RIGHT_OWN + RIGHT_BESIDE
PACK = 5
STEP = 20
CONTRACT = (((1,), (1,)), ((), ()))

LOAD, ROW_SENT, RELAY_IN, RELAY_SENT, ROW_IN = range(5)
RIGHT1_SENT, RIGHT1_IN, RIGHT2_SENT, RIGHT2_IN = range(4)
LEFT1_SENT, LEFT1_IN, LEFT2_SENT, LEFT2_IN = range(4, 8)
ROW_JOB, NEXT_JOB, PREV_JOB, FAR_JOB, BACK_JOB = range(5)
JOBS = 5


def flipped(block):
    half = block.shape[1] // 2
    return jnp.concatenate([block[:, half:], -block[:, :half]], axis=1)


def kernel(
    n_ka, row, cross, neighbour, shift_id, block_map, coeffs, out,
    shifts_out, shifts_in, table_rows, table, own, packed, right1, right2_0, right2_1, right2_2, right2_3, left1, left2,
    extra, extra_out, extra_via, relay, via, ahead,
    row_out, row_in, cross_out, cross_in, far_out, far_in, row_total, parts, inbox,
    chunk_sem, hop_sem, shift_sem, table_sem, via_sem, extra_sem, row_cross_sem, cross_sem,
    far_sem, result_sem,
):
    blocks = own.shape[0]
    bands = own.shape[1] // 2
    lanes = own.shape[2]
    deep = bands // CUTS
    right2 = (right2_0, right2_1, right2_2, right2_3)
    size = blocks // CHUNKS
    inside = blocks - cross
    ka = lax.axis_index("ka")
    ga = lax.axis_index("ga")
    other = 1 - ga
    core = lax.rem(ka, 2)
    place = lax.rem(ka, row)
    odd = lax.rem(place // 4, 2)
    aside = 4 - 8 * odd
    plane = lax.rem(ka // row + 2 * core + odd, 8)
    beside = lax.rem(ka // row + 2 * core + 1 - odd, 4)
    quad = lax.rem(plane, 4)
    half = plane // 4
    needs_row = (core == 0) | (place == row - 1)
    next_half = lax.rem(plane + 1, 8) // 4

    def at(step):
        return lax.rem(ka + n_ka + step, n_ka)

    def part(c):
        return pl.ds(c * size, size)

    def remote(source, target, sent, arrived, device):
        return pltpu.make_async_remote_copy(
            src_ref=source, dst_ref=target, send_sem=sent, recv_sem=arrived,
            device_id=device, device_id_type=MESH,
        )

    def load(c):
        return pltpu.make_async_copy(
            coeffs.at[part(c)], own.at[part(c)], chunk_sem.at[LOAD, c]
        )

    def row_direct(c):
        return remote(
            own.at[part(c)], ahead.at[part(c)],
            chunk_sem.at[ROW_SENT, c], chunk_sem.at[ROW_IN, c], (at(-1), ga),
        )

    def row_relayed(c):
        return remote(
            own.at[part(c)], relay.at[part(c)],
            chunk_sem.at[ROW_SENT, c], chunk_sem.at[RELAY_IN, c], (at(-1), other),
        )

    def relayed(c):
        return remote(
            relay.at[part(c)], ahead.at[part(c)],
            chunk_sem.at[RELAY_SENT, c], chunk_sem.at[ROW_IN, c], (ka, other),
        )

    def hop(source, target, sent, cut, step):
        return remote(
            source, target, hop_sem.at[sent, cut], hop_sem.at[sent + 1, cut], (at(step * row), ga)
        )

    def hop_right(cut):
        return hop(packed.at[half, cut], right1.at[cut], RIGHT1_SENT, cut, 1)

    def hop_left(cut):
        return hop(packed.at[1 - half, cut], left1.at[cut], LEFT1_SENT, cut, -1)

    def on_right(cut):
        return hop(right1.at[cut], right2[cut], RIGHT2_SENT, cut, 1)

    def on_left(cut):
        return hop(left1.at[cut], left2.at[cut], LEFT2_SENT, cut, -1)

    def hop_extra(turn):
        step = -1 if turn in LEFT else 1
        return remote(
            extra_out.at[turn], extra.at[turn],
            extra_sem.at[0, turn], extra_sem.at[1, turn], (at(step * row), ga),
        )

    def extra_aside(turn):
        return remote(
            extra_out.at[turn], extra_via.at[turn],
            extra_sem.at[0, turn], extra_sem.at[2, turn], (at(aside), ga),
        )

    def extra_back(turn):
        step = -1 if turn in LEFT else 1
        return remote(
            extra_via.at[turn], extra.at[turn],
            extra_sem.at[3, turn], extra_sem.at[1, turn], (at(aside + step * row), ga),
        )

    def to_via(c):
        return remote(
            own.at[part(c)], via, chunk_sem.at[ROW_SENT, c], via_sem.at[0], (at(2 * c), other)
        )

    def from_via():
        c = place // 2
        return remote(
            via, ahead.at[part(c)], via_sem.at[1], chunk_sem.at[ROW_IN, c],
            (at(-1 - place), other),
        )

    def swap_row():
        return remote(row_out, row_in, row_cross_sem.at[0], row_cross_sem.at[1], (ka, other))

    def swap(i):
        return remote(
            cross_out.at[i], cross_in.at[i], cross_sem.at[0, i], cross_sem.at[1, i], (ka, other)
        )

    def swap_far(i, cut):
        return remote(
            far_out.at[i, cut], far_in.at[i, cut],
            far_sem.at[0, i, cut], far_sem.at[1, i, cut], (ka, other),
        )

    def result(slot):
        job, step, same = RESULTS[slot]
        side = ga if same else other
        return remote(
            parts.at[job, side], inbox.at[slot],
            result_sem.at[0, slot], result_sem.at[1, slot], (at(step * row), side),
        )

    RESULTS = (
        (ROW_JOB, 0, False), (NEXT_JOB, 0, False),
        (PREV_JOB, -1, True), (PREV_JOB, -1, False),
        (FAR_JOB, -2, True), (FAR_JOB, -2, False),
        (BACK_JOB, 2, True), (BACK_JOB, 2, False),
    )

    def each(body):
        def run(c, carry):
            body(c)
            return carry
        lax.fori_loop(0, CHUNKS, run, 0)

    def bra_at(job, t):
        return table[job, t]

    def ket_at(job, t):
        return table[JOBS + job, t]

    def far_ket_at(job, t):
        return table[2 * JOBS + job, inside + t]

    def whole(source, index):
        return jnp.concatenate([source[cut, index] for cut in range(CUTS)], axis=0)

    def whole_far(index):
        return jnp.concatenate([right2[cut][index] for cut in range(CUTS)], axis=0)

    def gather(target, pick):
        def run(t, carry):
            for u in range(PACK):
                target[t * PACK + u] = pick(t * PACK + u)
            return carry
        lax.fori_loop(0, cross // PACK, run, 0)

    def whole_sum(total, bra, ket, count):
        def run(s, total):
            left = jnp.concatenate([bra(s * STEP + u) for u in range(STEP)], axis=1)
            right = jnp.concatenate([ket(s * STEP + u) for u in range(STEP)], axis=1)
            return total + lax.dot_general(
                left, right, CONTRACT, preferred_element_type=jnp.float32
            )
        return lax.fori_loop(0, count // STEP, run, total)

    def packed_sum(total, bra, ket, count):
        def run(s, total):
            left = jnp.concatenate([bra(s * STEP + u) for u in range(STEP)], axis=1)
            kets = [ket(s * STEP + u) for u in range(STEP)]
            right = jnp.concatenate(
                [jnp.concatenate(kets, axis=1),
                 jnp.concatenate([flipped(k) for k in kets], axis=1)], axis=0
            )
            return total + lax.dot_general(
                left, right, CONTRACT, preferred_element_type=jnp.float32
            )
        return lax.fori_loop(0, count // STEP, run, total)

    def keep(job, total):
        parts[job] = total.reshape(parts.shape[1:])

    zero = jnp.zeros((bands, 2 * bands), jnp.float32)

    each(lambda c: load(c).start())

    tile = (8, lanes)
    columns = neighbour.shape[1]
    targets = [jnp.broadcast_to(neighbour[:, b : b + 1], tile) for b in range(columns)]
    steps = (1, row, n_ka // 2)

    def shift_of(step):
        found = jnp.zeros(tile, jnp.int32)
        for b in range(columns):
            moved = jnp.broadcast_to(shift_id[:, b : b + 1], tile)
            found = found + jnp.where(targets[b] == at(step), moved, 0)
        return found

    row_shift, next_shift, far_shift = [shift_of(step) for step in steps]
    shifts_out[0] = next_shift
    shifts_out[1] = far_shift

    def send_shift(i):
        return remote(
            shifts_out.at[min(i, 1)], shifts_in.at[i],
            shift_sem.at[0, i], shift_sem.at[1, i], (at((row, 2 * row, -2 * row)[i]), ga),
        )

    barrier = pltpu.get_barrier_semaphore()
    meet = [
        (ka, other), (at(row), ga), (at(-row), ga), (at(row), other), (at(-row), other),
        (at(2 * row), ga), (at(-2 * row), ga), (at(2 * row), other), (at(-2 * row), other),
        (at(-1), jnp.where(core == 1, ga, other)), (at(1), jnp.where(core == 0, ga, other)),
        (at(aside), ga), (at(aside + row), ga), (at(aside - row), ga),
    ]
    paths = row // 2

    def greet(device):
        pl.semaphore_signal(barrier, inc=1, device_id=device, device_id_type=MESH)

    for device in meet:
        greet(device)

    @pl.when(place == 0)
    def _():
        for p in range(1, paths):
            greet((at(2 * p), other))

    @pl.when(place == row - 1)
    def _():
        for p in range(1, paths):
            greet((at(1 + 2 * p), other))

    between = (core == 0) & (place > 0)

    @pl.when(between)
    def _():
        greet((at(-place), other))
        greet((at(-1 - place), other))

    def pack_cut(cut):
        def pack(t, carry):
            for u in range(STEP):
                j = t * STEP + u
                real = own[j, pl.ds(cut * deep, deep), :]
                imag = own[j, pl.ds(bands + cut * deep, deep), :]
                mid = lanes // 2
                packed[0, cut, j] = jnp.concatenate([real[:, :mid], imag[:, :mid]], axis=1)
                packed[1, cut, j] = jnp.concatenate([real[:, mid:], imag[:, mid:]], axis=1)
            return carry
        lax.fori_loop(0, blocks // STEP, pack, 0)

    each(lambda c: load(c).wait())
    pack_cut(0)
    ends = (place == 0) | (place == row - 1)
    pl.semaphore_wait(
        barrier, len(meet) + jnp.where(ends, paths - 1, 0) + jnp.where(between, 2, 0)
    )
    for i in range(3):
        send_shift(i).start()

    def make_table():
        lane = lax.broadcasted_iota(jnp.int32, (lanes, lanes), 1)
        line = lax.broadcasted_iota(jnp.int32, (lanes, lanes), 0)
        maps = [
            jnp.concatenate(
                [block_map[:, a * blocks : (a + 1) * blocks],
                 jnp.zeros((block_map.shape[0], lanes - blocks), jnp.int32)], axis=1
            )
            for a in range(2)
        ]
        maps = [jnp.where(ga == a, maps[0], maps[1]) for a in range(2)]
        shifts = [row_shift, next_shift] + [shifts_in[i] for i in range(3)]
        choice = lax.broadcasted_iota(jnp.int32, tile, 0)
        rows = [
            jnp.sum(jnp.where(shift == choice, each_map, 0), axis=0, keepdims=True)
            for each_map in maps for shift in shifts
        ]
        rows = jnp.concatenate(rows + [jnp.zeros((16 - 2 * JOBS, lanes), jnp.int32)], axis=0)
        number = lax.broadcasted_iota(jnp.int32, rows.shape, 0)
        spot = lax.broadcasted_iota(jnp.int32, rows.shape, 1)
        source = jnp.where(rows >= blocks, 1, 0)
        same = jnp.where(source == jnp.where(number < JOBS, ga, other), 1, 0)
        local = rows - blocks * source
        same_t = same.T
        kept = [
            jnp.sum(jnp.where(line < lane, same_t[:, r : r + 1], 0), axis=0, keepdims=True)
            for r in range(2 * JOBS)
        ]
        kept = jnp.concatenate(kept + [jnp.zeros((16 - 2 * JOBS, lanes), jnp.int32)], axis=0)
        rank = jnp.where(same == 1, kept, inside + spot - kept)
        rank_t = jnp.where(spot < blocks, rank, -1).T
        local_t = local.T
        hits = [rank_t[:, r : r + 1] == lane for r in range(2 * JOBS)]
        lists = [jnp.sum(jnp.where(hits[r], line, 0), axis=0, keepdims=True) for r in range(JOBS)]
        lists += [
            jnp.sum(jnp.where(hits[r], local_t[:, r : r + 1], 0), axis=0, keepdims=True)
            for r in range(2 * JOBS)
        ]
        lists += [jnp.zeros((1, lanes), jnp.int32)]
        table_rows[...] = jnp.concatenate(lists, axis=0)

    def first_sends(c):
        @pl.when(core == 1)
        def _():
            row_direct(c).start()

        @pl.when((core == 0) & ((place > 0) | (c == 0)))
        def _():
            row_relayed(c).start()

        @pl.when((place == 0) & (c > 0))
        def _():
            to_via(c).start()

    each(first_sends)
    hop_right(0).start()
    hop_left(0).start()
    pack_cut(1)
    for cut in range(1, CUTS):
        if cut + 1 < CUTS:
            pack_cut(cut + 1)
        hop_right(cut).start()
        hop_left(cut).start()
    for i in range(3):
        send_shift(i).wait_recv()
    make_table()
    fetch = pltpu.make_async_copy(table_rows, table, table_sem)
    fetch.start()
    fetch.wait()
    gather(cross_out.at[0], lambda t: whole(packed.at[1 - next_half], bra_at(NEXT_JOB, inside + t)))
    gather(cross_out.at[1], lambda t: whole(packed.at[half], far_ket_at(PREV_JOB, t)))

    @pl.when(needs_row)
    def _():
        gather(row_out, lambda t: own[bra_at(ROW_JOB, inside + t)])
        swap_row().start()

    swap(0).start()
    swap(1).start()

    @pl.when(quad == 3)
    def _():
        for turn in RIGHT_BESIDE + RIGHT_OWN:
            gather(
                extra_out.at[turn],
                lambda t: whole(packed.at[1 - half], bra_at(NEXT_JOB, turn * cross + t)),
            )
        for turn in RIGHT_BESIDE:
            extra_aside(turn).start()

    @pl.when(quad == 0)
    def _():
        for turn in LEFT_BESIDE + LEFT_OWN:
            gather(
                extra_out.at[turn],
                lambda t: whole(packed.at[half], ket_at(PREV_JOB, turn * cross + t)),
            )
        for turn in LEFT_BESIDE:
            extra_aside(turn).start()

    def relay_on(c):
        row_relayed(c).wait_recv()
        relayed(c).start()

    for cut in range(CUTS):
        hop_right(cut).wait_recv()
        on_right(cut).start()
        hop_left(cut).wait_recv()

        @pl.when(between & ((place - 2) // 4 == cut))
        def _():
            to_via(0).wait_recv()
            from_via().start()

        on_left(cut).start()

        @pl.when((core == 1) & (place < row - 1))
        def _(cut=cut):
            for c in range(cut * CHUNKS // CUTS, (cut + 1) * CHUNKS // CUTS):
                relay_on(c)

        if cut == 1:
            @pl.when(place == row - 1)
            def _():
                relay_on(0)

    @pl.when(quad == 3)
    def _():
        for turn in RIGHT_OWN:
            hop_extra(turn).start()

    @pl.when(quad == 0)
    def _():
        for turn in LEFT_OWN:
            hop_extra(turn).start()

    @pl.when(beside == 3)
    def _():
        for turn in RIGHT_BESIDE:
            extra_aside(turn).wait_recv()
            extra_back(turn).start()

    @pl.when(beside == 0)
    def _():
        for turn in LEFT_BESIDE:
            extra_aside(turn).wait_recv()
            extra_back(turn).start()

    swap(0).wait_recv()
    total = packed_sum(
        zero,
        lambda t: whole(packed.at[1 - next_half], bra_at(NEXT_JOB, t)),
        lambda t: whole(left1, ket_at(NEXT_JOB, t)),
        inside,
    )
    total = packed_sum(
        total, lambda t: cross_in[0, t], lambda t: whole(left1, far_ket_at(NEXT_JOB, t)), cross
    )
    keep(NEXT_JOB, total)

    swap(1).wait_recv()

    @pl.when(quad != 0)
    def _():
        total = packed_sum(
            zero,
            lambda t: whole(right1, bra_at(PREV_JOB, t)),
            lambda t: whole(packed.at[half], ket_at(PREV_JOB, t)),
            inside,
        )
        total = packed_sum(
            total,
            lambda t: whole(right1, bra_at(PREV_JOB, inside + t)),
            lambda t: cross_in[1, t],
            cross,
        )
        keep(PREV_JOB, total)

    @pl.when(quad != 3)
    def _():
        result(1).start()

    def along_row():
        each(lambda c: row_direct(c).wait_recv())
        row_total[...] = whole_sum(
            jnp.zeros(row_total.shape, jnp.float32),
            lambda t: own[bra_at(ROW_JOB, t)],
            lambda t: ahead[ket_at(ROW_JOB, t)],
            inside,
        )

        @pl.when(needs_row)
        def _():
            swap_row().wait_recv()
            row_total[...] = whole_sum(
                row_total[...], lambda t: row_in[t], lambda t: ahead[far_ket_at(ROW_JOB, t)], cross
            )

        @pl.when(jnp.logical_not(needs_row))
        def _():
            row_total[...] = whole_sum(
                row_total[...],
                lambda t: own[bra_at(ROW_JOB, inside + t)],
                lambda t: relay[ket_at(ROW_JOB, inside + t)],
                cross,
            )

        lower = row_total[pl.ds(bands, bands)]
        keep(
            ROW_JOB,
            row_total[pl.ds(0, bands)]
            + jnp.concatenate([lower[:, bands:], -lower[:, :bands]], axis=1),
        )
        result(0).start()

    @pl.when(core == 0)
    def _():
        along_row()

    def far_swaps(cut):
        on_right(cut).wait_recv()
        gather(far_out.at[0, cut], lambda t: right2[cut][bra_at(FAR_JOB, inside + t)])
        gather(far_out.at[1, cut], lambda t: right2[cut][far_ket_at(BACK_JOB, t)])
        swap_far(0, cut).start()
        swap_far(1, cut).start()

    far_swaps(0)

    @pl.when(quad != 0)
    def _():
        result(2).start()
        result(3).start()

    for cut in range(1, CUTS):
        far_swaps(cut)

    for cut in range(CUTS):
        on_left(cut).wait_recv()
    far = packed_sum(
        zero,
        lambda t: whole_far(bra_at(FAR_JOB, t)),
        lambda t: whole(left2, ket_at(FAR_JOB, t)),
        inside,
    )
    back = packed_sum(
        zero,
        lambda t: whole(left2, bra_at(BACK_JOB, t)),
        lambda t: whole_far(ket_at(BACK_JOB, t)),
        inside,
    )

    @pl.when(core == 1)
    def _():
        along_row()

    for cut in range(CUTS):
        swap_far(0, cut).wait_recv()
        swap_far(1, cut).wait_recv()
    far = packed_sum(
        far,
        lambda t: whole(far_in.at[0], t),
        lambda t: whole(left2, far_ket_at(FAR_JOB, t)),
        cross,
    )
    keep(FAR_JOB, far)
    back = packed_sum(
        back,
        lambda t: whole(left2, bra_at(BACK_JOB, inside + t)),
        lambda t: whole(far_in.at[1], t),
        cross,
    )
    keep(BACK_JOB, back)
    for slot in (4, 5, 6, 7):
        result(slot).start()

    @pl.when(quad == 3)
    def _():
        more = zero
        for turn in LEFT:
            hop_extra(turn).wait_recv()
            more = packed_sum(
                more,
                lambda t: whole(packed.at[1 - half], bra_at(NEXT_JOB, turn * cross + t)),
                lambda t: extra[turn, t],
                cross,
            )
        keep(NEXT_JOB, parts[NEXT_JOB].reshape(zero.shape) + more)
        result(1).start()

    @pl.when(quad == 0)
    def _():
        total = zero
        for turn in RIGHT:
            hop_extra(turn).wait_recv()
            total = packed_sum(
                total,
                lambda t: extra[turn, t],
                (lambda t: whole(packed.at[half], ket_at(PREV_JOB, turn * cross + t)))
                if turn * cross < inside else (lambda t: cross_in[1, t]),
                cross,
            )
        keep(PREV_JOB, total)
        result(2).start()
        result(3).start()

    for slot in range(len(RESULTS)):
        result(slot).wait_recv()
    found = [
        parts[ROW_JOB, ga] + inbox[0],
        (parts[NEXT_JOB, ga] + inbox[1]) + (inbox[2] + inbox[3]),
        (inbox[4] + inbox[5]) + (inbox[6] + inbox[7]),
    ]
    for b in range(columns):
        target = jnp.broadcast_to(neighbour[:, b : b + 1], found[0].shape)
        chosen = jnp.where(
            target == at(steps[0]), found[0], jnp.where(target == at(steps[1]), found[1], found[2])
        )
        out[b, 0] = chosen[:, :bands]
        out[b, 1] = chosen[:, bands:]

    def drain(c):
        row_direct(c).wait_send()

        @pl.when((core == 1) & ((place < row - 1) | (c == 0)))
        def _():
            relayed(c).wait_send()

    each(drain)
    for cut in range(CUTS):
        hop_right(cut).wait_send()
        hop_left(cut).wait_send()
        on_right(cut).wait_send()
        on_left(cut).wait_send()
        swap_far(0, cut).wait_send()
        swap_far(1, cut).wait_send()
    for i in range(3):
        send_shift(i).wait_send()

    @pl.when(quad == 3)
    def _():
        for turn in RIGHT:
            hop_extra(turn).wait_send()

    @pl.when(quad == 0)
    def _():
        for turn in LEFT:
            hop_extra(turn).wait_send()

    @pl.when(beside == 3)
    def _():
        for turn in RIGHT_BESIDE:
            extra_back(turn).wait_send()

    @pl.when(beside == 0)
    def _():
        for turn in LEFT_BESIDE:
            extra_back(turn).wait_send()

    @pl.when(between)
    def _():
        from_via().wait_send()


    @pl.when(needs_row)
    def _():
        swap_row().wait_send()

    for i in range(2):
        swap(i).wait_send()
    for slot in range(len(RESULTS)):
        result(slot).wait_send()


def on_device(coeffs, neighbour, shift_id, block_map):
    _, blocks, _, bands, lanes = coeffs.shape
    columns = neighbour.shape[1]
    n_ka = lax.axis_size("ka")
    row = n_ka // 8
    cross = 2 * max(1, blocks // 12)
    def half_buffer(*lead):
        return pltpu.VMEM((*lead, bands, lanes), jnp.bfloat16)

    def cut_buffer(*lead):
        return pltpu.VMEM((*lead, bands // CUTS, lanes), jnp.bfloat16)

    def whole_buffer(*lead):
        return pltpu.VMEM((*lead, 2 * bands, lanes), jnp.bfloat16)

    found = pl.pallas_call(
        functools.partial(kernel, n_ka, row, cross),
        out_shape=jax.ShapeDtypeStruct((columns, 2, bands // 2, bands), jnp.float32),
        in_specs=[
            pl.BlockSpec(memory_space=pltpu.VMEM),
            pl.BlockSpec(memory_space=pltpu.VMEM),
            pl.BlockSpec(memory_space=pltpu.VMEM),
            pl.BlockSpec(memory_space=pl.ANY),
        ],
        out_specs=pl.BlockSpec(memory_space=pltpu.VMEM),
        scratch_shapes=[
            pltpu.VMEM((2, 8, lanes), jnp.int32),
            pltpu.VMEM((3, 8, lanes), jnp.int32),
            pltpu.VMEM((16, lanes), jnp.int32),
            pltpu.SMEM((16, lanes), jnp.int32),
            whole_buffer(blocks),
            cut_buffer(2, CUTS, blocks),
            cut_buffer(CUTS, blocks),
            *[cut_buffer(blocks) for _ in range(CUTS)],
            cut_buffer(CUTS, blocks), cut_buffer(CUTS, blocks),
            half_buffer(TURNS, cross), half_buffer(TURNS, cross), half_buffer(TURNS, cross),
            whole_buffer(blocks), whole_buffer(blocks // CHUNKS), whole_buffer(blocks),
            whole_buffer(cross), whole_buffer(cross),
            half_buffer(2, cross), half_buffer(2, cross),
            cut_buffer(2, CUTS, cross), cut_buffer(2, CUTS, cross),
            pltpu.VMEM((2 * bands, 2 * bands), jnp.float32),
            pltpu.VMEM((5, 2, bands // 2, 2 * bands), jnp.float32),
            pltpu.VMEM((8, bands // 2, 2 * bands), jnp.float32),
            pltpu.SemaphoreType.DMA((5, CHUNKS)),
            pltpu.SemaphoreType.DMA((8, CUTS)),
            pltpu.SemaphoreType.DMA((2, 3)),
            pltpu.SemaphoreType.DMA,
            pltpu.SemaphoreType.DMA((2,)),
            pltpu.SemaphoreType.DMA((4, TURNS)),
            pltpu.SemaphoreType.DMA((2,)),
            pltpu.SemaphoreType.DMA((2, 2)),
            pltpu.SemaphoreType.DMA((2, 2, CUTS)),
            pltpu.SemaphoreType.DMA((2, 8)),
        ],
        compiler_params=pltpu.CompilerParams(
            collective_id=0, has_side_effects=True, vmem_limit_bytes=61 * 2**20
        ),
        name="overlaps",
    )(neighbour, shift_id, block_map, coeffs.reshape(blocks, 2 * bands, lanes))
    return found[None]


def solution(mesh):
    in_specs = (P("ka", "ga", None, None, None), P("ka", None), P("ka", None), P())
    out_specs = P("ka", None, None, "ga", None)
    return jax.shard_map(
        on_device, mesh=mesh, in_specs=in_specs, out_specs=out_specs, check_vma=False
    )
```

time: 130 us -> 117 us (0.900)
  the two profiles are of different devices: /device:TPU:98 before, /device:TPU:2 now
where the time goes in v3:
time: 117 us; the launch traced here: 114 us
  Pallas kernels  113 us (97%)
  local copies, waits for them, and re-layouts  1.54 us (1%)
    pallas_call x1, Pallas kernels, on_device(): pl.pallas_call(functools.partial(kernel, n_ka, row, cross), out_shape=jax...  113 us

profile of v3, /device:TPU:2, one launch (start us, length us, event | category | flops | bytes accessed | tf_op | source)
XLA Modules:
  0.0 114.3 jit_solution(2544239445849060182)
XLA Ops:
  0.0 112.8 %overlaps.1 = f32[3,2,32,64]{3,2,1,0:T(8,128)} custom-call(s32[1,3]{1,0:T(1,128)} %neighbour.1, s32[1,3]{1,0:T(1,128)} %shift_id.1, s32[8,240]{1,0:T(8,128)} %block_map.1, bf16[120,128,128]{2,1,0:T(8,128)(2,1)} %bitcast.2), custom_call_target="tpu_custom_call" | custom-call | tf_op jit(solution)/shard_map/overlaps/pallas_call | solution.py:696
  112.8 1.5 %copy.6 = f32[1,3,2,32,64]{4,3,2,1,0:T(8,128)} copy(f32[1,3,2,32,64]{4,3,2,1,0:T(8,128)} %bitcast.3) | data formatting | bytes 98304

commit v4 on v3

--- a/solution.py
+++ b/solution.py
@@ -11,10 +11,7 @@
 CHUNKS = 8
 CUTS = 4
 TURNS = 6
-LEFT_OWN, LEFT_BESIDE = (0,), (1,)
-RIGHT_OWN, RIGHT_BESIDE = (2, 3), (4, 5)
-LEFT = LEFT_OWN + LEFT_BESIDE
-RIGHT = RIGHT_OWN + RIGHT_BESIDE
+OWN_TURNS, ASIDE_TURNS = (0, 1, 2), (3, 4, 5)
 PACK = 5
 STEP = 20
 CONTRACT = (((1,), (1,)), ((), ()))
@@ -34,7 +31,7 @@
 def kernel(
     n_ka, row, cross, neighbour, shift_id, block_map, coeffs, out,
     shifts_out, shifts_in, table_rows, table, own, packed, right1, right2_0, right2_1, right2_2, right2_3, left1, left2,
-    extra, extra_out, extra_via, relay, via, ahead,
+    extra, extra_out, extra_via, relay, via, via_below, ahead,
     row_out, row_in, cross_out, cross_in, far_out, far_in, row_total, parts, inbox,
     chunk_sem, hop_sem, shift_sem, table_sem, via_sem, extra_sem, row_cross_sem, cross_sem,
     far_sem, result_sem,
@@ -72,9 +69,10 @@
             device_id=device, device_id_type=MESH,
         )
 
-    def load(c):
+    def load(i):
+        lines = pl.ds((i // 2 + lax.rem(i, 2) * CUTS) * deep, deep)
         return pltpu.make_async_copy(
-            coeffs.at[part(c)], own.at[part(c)], chunk_sem.at[LOAD, c]
+            coeffs.at[:, lines], own.at[:, lines], chunk_sem.at[LOAD, i]
         )
 
     def row_direct(c):
@@ -113,10 +111,9 @@
         return hop(left1.at[cut], left2.at[cut], LEFT2_SENT, cut, -1)
 
     def hop_extra(turn):
-        step = -1 if turn in LEFT else 1
         return remote(
             extra_out.at[turn], extra.at[turn],
-            extra_sem.at[0, turn], extra_sem.at[1, turn], (at(step * row), ga),
+            extra_sem.at[0, turn], extra_sem.at[1, turn], (at(row), ga),
         )
 
     def extra_aside(turn):
@@ -126,22 +123,28 @@
         )
 
     def extra_back(turn):
-        step = -1 if turn in LEFT else 1
         return remote(
             extra_via.at[turn], extra.at[turn],
-            extra_sem.at[3, turn], extra_sem.at[1, turn], (at(aside + step * row), ga),
-        )
+            extra_sem.at[3, turn], extra_sem.at[1, turn], (at(aside + row), ga),
+        )
+
+    def via_side(c):
+        return jnp.where(lax.rem(c, 2) == 1, other, ga)
 
     def to_via(c):
         return remote(
-            own.at[part(c)], via, chunk_sem.at[ROW_SENT, c], via_sem.at[0], (at(2 * c), other)
-        )
+            own.at[part(c)], via, chunk_sem.at[ROW_SENT, c], via_sem.at[0],
+            (at(2 * c), via_side(c)),
+        )
+
+    def down_via():
+        return remote(via, via_below, via_sem.at[1], via_sem.at[2], (at(-row), ga))
 
     def from_via():
         c = place // 2
         return remote(
-            via, ahead.at[part(c)], via_sem.at[1], chunk_sem.at[ROW_IN, c],
-            (at(-1 - place), other),
+            via_below, ahead.at[part(c)], via_sem.at[3], chunk_sem.at[ROW_IN, c],
+            (at(row - 1 - place), via_side(c)),
         )
 
     def swap_row():
@@ -270,19 +273,23 @@
     @pl.when(place == 0)
     def _():
         for p in range(1, paths):
-            greet((at(2 * p), other))
+            greet((at(2 * p), via_side(p)))
 
     @pl.when(place == row - 1)
     def _():
         for p in range(1, paths):
-            greet((at(1 + 2 * p), other))
+            greet((at(1 - row + 2 * p), via_side(p)))
 
     between = (core == 0) & (place > 0)
 
     @pl.when(between)
     def _():
-        greet((at(-place), other))
-        greet((at(-1 - place), other))
+        greet((at(-place), via_side(place // 2)))
+        greet((at(row - 1 - place), via_side(place // 2)))
+
+    def load_cut(cut):
+        load(2 * cut).wait()
+        load(2 * cut + 1).wait()
 
     def pack_cut(cut):
         def pack(t, carry):
@@ -296,7 +303,7 @@
             return carry
         lax.fori_loop(0, blocks // STEP, pack, 0)
 
-    each(lambda c: load(c).wait())
+    load_cut(0)
     pack_cut(0)
     ends = (place == 0) | (place == row - 1)
     pl.semaphore_wait(
@@ -359,9 +366,11 @@
         def _():
             to_via(c).start()
 
-    each(first_sends)
     hop_right(0).start()
     hop_left(0).start()
+    for cut in range(1, CUTS):
+        load_cut(cut)
+    each(first_sends)
     pack_cut(1)
     for cut in range(1, CUTS):
         if cut + 1 < CUTS:
@@ -387,22 +396,12 @@
 
     @pl.when(quad == 3)
     def _():
-        for turn in RIGHT_BESIDE + RIGHT_OWN:
+        for turn in ASIDE_TURNS + OWN_TURNS:
             gather(
                 extra_out.at[turn],
                 lambda t: whole(packed.at[1 - half], bra_at(NEXT_JOB, turn * cross + t)),
             )
-        for turn in RIGHT_BESIDE:
-            extra_aside(turn).start()
-
-    @pl.when(quad == 0)
-    def _():
-        for turn in LEFT_BESIDE + LEFT_OWN:
-            gather(
-                extra_out.at[turn],
-                lambda t: whole(packed.at[half], ket_at(PREV_JOB, turn * cross + t)),
-            )
-        for turn in LEFT_BESIDE:
+        for turn in ASIDE_TURNS:
             extra_aside(turn).start()
 
     def relay_on(c):
@@ -414,10 +413,11 @@
         on_right(cut).start()
         hop_left(cut).wait_recv()
 
-        @pl.when(between & ((place - 2) // 4 == cut))
-        def _():
-            to_via(0).wait_recv()
-            from_via().start()
+        if cut == 1:
+            @pl.when(between)
+            def _():
+                to_via(0).wait_recv()
+                down_via().start()
 
         on_left(cut).start()
 
@@ -433,23 +433,12 @@
 
     @pl.when(quad == 3)
     def _():
-        for turn in RIGHT_OWN:
+        for turn in OWN_TURNS:
             hop_extra(turn).start()
 
-    @pl.when(quad == 0)
-    def _():
-        for turn in LEFT_OWN:
-            hop_extra(turn).start()
-
     @pl.when(beside == 3)
     def _():
-        for turn in RIGHT_BESIDE:
-            extra_aside(turn).wait_recv()
-            extra_back(turn).start()
-
-    @pl.when(beside == 0)
-    def _():
-        for turn in LEFT_BESIDE:
+        for turn in ASIDE_TURNS:
             extra_aside(turn).wait_recv()
             extra_back(turn).start()
 
@@ -483,9 +472,7 @@
         )
         keep(PREV_JOB, total)
 
-    @pl.when(quad != 3)
-    def _():
-        result(1).start()
+    result(1).start()
 
     def along_row():
         each(lambda c: row_direct(c).wait_recv())
@@ -533,71 +520,27 @@
 
     far_swaps(0)
 
+    @pl.when(between)
+    def _():
+        down_via().wait_recv()
+        from_via().start()
+
     @pl.when(quad != 0)
     def _():
         result(2).start()
         result(3).start()
 
     for cut in range(1, CUTS):
+        if cut == CUTS - 1:
+            @pl.when((core == 1) & (place > 1))
+            def _():
+                along_row()
+
         far_swaps(cut)
 
-    for cut in range(CUTS):
-        on_left(cut).wait_recv()
-    far = packed_sum(
-        zero,
-        lambda t: whole_far(bra_at(FAR_JOB, t)),
-        lambda t: whole(left2, ket_at(FAR_JOB, t)),
-        inside,
-    )
-    back = packed_sum(
-        zero,
-        lambda t: whole(left2, bra_at(BACK_JOB, t)),
-        lambda t: whole_far(ket_at(BACK_JOB, t)),
-        inside,
-    )
-
-    @pl.when(core == 1)
-    def _():
-        along_row()
-
-    for cut in range(CUTS):
-        swap_far(0, cut).wait_recv()
-        swap_far(1, cut).wait_recv()
-    far = packed_sum(
-        far,
-        lambda t: whole(far_in.at[0], t),
-        lambda t: whole(left2, far_ket_at(FAR_JOB, t)),
-        cross,
-    )
-    keep(FAR_JOB, far)
-    back = packed_sum(
-        back,
-        lambda t: whole(left2, bra_at(BACK_JOB, inside + t)),
-        lambda t: whole(far_in.at[1], t),
-        cross,
-    )
-    keep(BACK_JOB, back)
-    for slot in (4, 5, 6, 7):
-        result(slot).start()
-
-    @pl.when(quad == 3)
-    def _():
-        more = zero
-        for turn in LEFT:
-            hop_extra(turn).wait_recv()
-            more = packed_sum(
-                more,
-                lambda t: whole(packed.at[1 - half], bra_at(NEXT_JOB, turn * cross + t)),
-                lambda t: extra[turn, t],
-                cross,
-            )
-        keep(NEXT_JOB, parts[NEXT_JOB].reshape(zero.shape) + more)
-        result(1).start()
-
-    @pl.when(quad == 0)
-    def _():
+    def previous_extra():
         total = zero
-        for turn in RIGHT:
+        for turn in range(TURNS):
             hop_extra(turn).wait_recv()
             total = packed_sum(
                 total,
@@ -610,6 +553,50 @@
         result(2).start()
         result(3).start()
 
+    for cut in range(CUTS):
+        on_left(cut).wait_recv()
+    far = packed_sum(
+        zero,
+        lambda t: whole_far(bra_at(FAR_JOB, t)),
+        lambda t: whole(left2, ket_at(FAR_JOB, t)),
+        inside,
+    )
+    back = packed_sum(
+        zero,
+        lambda t: whole(left2, bra_at(BACK_JOB, t)),
+        lambda t: whole_far(ket_at(BACK_JOB, t)),
+        inside,
+    )
+
+
+    @pl.when(place == 1)
+    def _():
+        along_row()
+
+    for cut in range(CUTS):
+        swap_far(0, cut).wait_recv()
+        swap_far(1, cut).wait_recv()
+    far = packed_sum(
+        far,
+        lambda t: whole(far_in.at[0], t),
+        lambda t: whole(left2, far_ket_at(FAR_JOB, t)),
+        cross,
+    )
+    keep(FAR_JOB, far)
+    back = packed_sum(
+        back,
+        lambda t: whole(left2, bra_at(BACK_JOB, inside + t)),
+        lambda t: whole(far_in.at[1], t),
+        cross,
+    )
+    keep(BACK_JOB, back)
+    for slot in (4, 5, 6, 7):
+        result(slot).start()
+
+    @pl.when(quad == 0)
+    def _():
+        previous_extra()
+
     for slot in range(len(RESULTS)):
         result(slot).wait_recv()
     found = [
@@ -645,26 +632,17 @@
 
     @pl.when(quad == 3)
     def _():
-        for turn in RIGHT:
+        for turn in range(TURNS):
             hop_extra(turn).wait_send()
 
-    @pl.when(quad == 0)
-    def _():
-        for turn in LEFT:
-            hop_extra(turn).wait_send()
-
     @pl.when(beside == 3)
     def _():
-        for turn in RIGHT_BESIDE:
+        for turn in ASIDE_TURNS:
             extra_back(turn).wait_send()
 
-    @pl.when(beside == 0)
-    def _():
-        for turn in LEFT_BESIDE:
-            extra_back(turn).wait_send()
-
     @pl.when(between)
     def _():
+        down_via().wait_send()
         from_via().wait_send()
 
 
@@ -714,7 +692,7 @@
             *[cut_buffer(blocks) for _ in range(CUTS)],
             cut_buffer(CUTS, blocks), cut_buffer(CUTS, blocks),
             half_buffer(TURNS, cross), half_buffer(TURNS, cross), half_buffer(TURNS, cross),
-            whole_buffer(blocks), whole_buffer(blocks // CHUNKS), whole_buffer(blocks),
+            whole_buffer(blocks), whole_buffer(blocks // CHUNKS), whole_buffer(blocks // CHUNKS), whole_buffer(blocks),
             whole_buffer(cross), whole_buffer(cross),
             half_buffer(2, cross), half_buffer(2, cross),
             cut_buffer(2, CUTS, cross), cut_buffer(2, CUTS, cross),
@@ -725,7 +703,7 @@
             pltpu.SemaphoreType.DMA((8, CUTS)),
             pltpu.SemaphoreType.DMA((2, 3)),
             pltpu.SemaphoreType.DMA,
-            pltpu.SemaphoreType.DMA((2,)),
+            pltpu.SemaphoreType.DMA((4,)),
             pltpu.SemaphoreType.DMA((4, TURNS)),
             pltpu.SemaphoreType.DMA((2,)),
             pltpu.SemaphoreType.DMA((2, 2)),

time: 117 us -> 113 us (0.966); the launches traced: 114 us -> 113 us
  Pallas kernels: 113 us -> 111 us
    pallas_call x1, Pallas kernels: 113 us -> 111 us  [on_device(): pl.pallas_call(functools.partial(kernel, n_ka, row, cross), out_shape=jax...]
where the time goes in v4:
time: 113 us
  Pallas kernels  111 us (98%)
  local copies, waits for them, and re-layouts  1.54 us (1%)
    pallas_call x1, Pallas kernels, on_device(): pl.pallas_call(functools.partial(kernel, n_ka, row, cross), out_shape=jax...  111 us

profile of v4, /device:TPU:2, one launch (start us, length us, event | category | flops | bytes accessed | tf_op | source)
XLA Modules:
  0.0 112.9 jit_solution(224509815242080280)
XLA Ops:
  0.0 111.3 %overlaps.1 = f32[3,2,32,64]{3,2,1,0:T(8,128)} custom-call(s32[1,3]{1,0:T(1,128)} %neighbour.1, s32[1,3]{1,0:T(1,128)} %shift_id.1, s32[8,240]{1,0:T(8,128)} %block_map.1, bf16[120,128,128]{2,1,0:T(8,128)(2,1)} %bitcast.2), custom_call_target="tpu_custom_call" | custom-call | tf_op jit(solution)/shard_map/overlaps/pallas_call | solution.py:674
  111.4 1.5 %copy.6 = f32[1,3,2,32,64]{4,3,2,1,0:T(8,128)} copy(f32[1,3,2,32,64]{4,3,2,1,0:T(8,128)} %bitcast.3) | data formatting | bytes 98304

commit v5 on v3

--- a/solution.py
+++ b/solution.py
@@ -11,10 +11,10 @@
 CHUNKS = 8
 CUTS = 4
 TURNS = 6
-LEFT_OWN, LEFT_BESIDE = (0,), (1,)
-RIGHT_OWN, RIGHT_BESIDE = (2, 3), (4, 5)
-LEFT = LEFT_OWN + LEFT_BESIDE
-RIGHT = RIGHT_OWN + RIGHT_BESIDE
+LEFT_OWN, LEFT_ASIDE = (0,), (1,)
+RIGHT_OWN, RIGHT_ASIDE = (2, 3), (4, 5)
+LEFT = LEFT_OWN + LEFT_ASIDE
+RIGHT = RIGHT_OWN + RIGHT_ASIDE
 PACK = 5
 STEP = 20
 CONTRACT = (((1,), (1,)), ((), ()))
@@ -22,8 +22,8 @@
 LOAD, ROW_SENT, RELAY_IN, RELAY_SENT, ROW_IN = range(5)
 RIGHT1_SENT, RIGHT1_IN, RIGHT2_SENT, RIGHT2_IN = range(4)
 LEFT1_SENT, LEFT1_IN, LEFT2_SENT, LEFT2_IN = range(4, 8)
-ROW_JOB, NEXT_JOB, PREV_JOB, FAR_JOB, BACK_JOB = range(5)
-JOBS = 5
+ROW_JOB, NEXT_JOB, PREV_JOB, FAR_JOB, BACK_JOB, WRAP_JOB = range(6)
+JOBS = 6
 
 
 def flipped(block):
@@ -32,11 +32,11 @@
 
 
 def kernel(
-    n_ka, row, cross, neighbour, shift_id, block_map, coeffs, out,
-    shifts_out, shifts_in, table_rows, table, own, packed, right1, right2_0, right2_1, right2_2, right2_3, left1, left2,
-    extra, extra_out, extra_via, relay, via, ahead,
+    n_ka, row, cross, neighbour_in, shift_in, map_in, coeffs, out,
+    neighbour, shift_id, block_map,    shifts_out, shifts_in, table_rows, table, own, packed, right1, right2_0, right2_1, right2_2, right2_3, left1, left2,
+    extra, extra_out, extra_via, relay, ahead, near, pass_a, pass_b, wrap_out, wrap_in,
     row_out, row_in, cross_out, cross_in, far_out, far_in, row_total, parts, inbox,
-    chunk_sem, hop_sem, shift_sem, table_sem, via_sem, extra_sem, row_cross_sem, cross_sem,
+    small_sem, chunk_sem, hop_sem, shift_sem, table_sem, near_sem, wrap_sem, extra_sem, row_cross_sem, cross_sem,
     far_sem, result_sem,
 ):
     blocks = own.shape[0]
@@ -53,11 +53,14 @@
     place = lax.rem(ka, row)
     odd = lax.rem(place // 4, 2)
     aside = 4 - 8 * odd
-    plane = lax.rem(ka // row + 2 * core + odd, 8)
-    beside = lax.rem(ka // row + 2 * core + 1 - odd, 4)
+    turned = jnp.where(odd == 1, 3 - 2 * core, 2 * core)
+    plane = lax.rem(ka // row + turned, 8)
+    beside = lax.rem(ka // row + 3 - turned, 4)
+    first = place == 0
+    last = place == row - 1
     quad = lax.rem(plane, 4)
     half = plane // 4
-    needs_row = (core == 0) | (place == row - 1)
+    needs_row = (core == 0) | last
     next_half = lax.rem(plane + 1, 8) // 4
 
     def at(step):
@@ -72,9 +75,10 @@
             device_id=device, device_id_type=MESH,
         )
 
-    def load(c):
+    def load(i):
+        lines = pl.ds((i // 2 + lax.rem(i, 2) * CUTS) * deep, deep)
         return pltpu.make_async_copy(
-            coeffs.at[part(c)], own.at[part(c)], chunk_sem.at[LOAD, c]
+            coeffs.at[:, lines], own.at[:, lines], chunk_sem.at[LOAD, i]
         )
 
     def row_direct(c):
@@ -113,10 +117,10 @@
         return hop(left1.at[cut], left2.at[cut], LEFT2_SENT, cut, -1)
 
     def hop_extra(turn):
-        step = -1 if turn in LEFT else 1
         return remote(
             extra_out.at[turn], extra.at[turn],
-            extra_sem.at[0, turn], extra_sem.at[1, turn], (at(step * row), ga),
+            extra_sem.at[0, turn], extra_sem.at[1, turn],
+            (at(-row if turn in LEFT else row), ga),
         )
 
     def extra_aside(turn):
@@ -126,23 +130,37 @@
         )
 
     def extra_back(turn):
-        step = -1 if turn in LEFT else 1
         return remote(
             extra_via.at[turn], extra.at[turn],
-            extra_sem.at[3, turn], extra_sem.at[1, turn], (at(aside + step * row), ga),
-        )
-
-    def to_via(c):
-        return remote(
-            own.at[part(c)], via, chunk_sem.at[ROW_SENT, c], via_sem.at[0], (at(2 * c), other)
-        )
-
-    def from_via():
-        c = place // 2
-        return remote(
-            via, ahead.at[part(c)], via_sem.at[1], chunk_sem.at[ROW_IN, c],
-            (at(-1 - place), other),
-        )
+            extra_sem.at[3, turn], extra_sem.at[1, turn],
+            (at(aside + (-row if turn in LEFT else row)), ga),
+        )
+
+    def carry_left(cut):
+        return remote(
+            left1.at[cut], pass_a.at[cut],
+            near_sem.at[0, cut], near_sem.at[1, cut], (at(row - 1), other),
+        )
+
+    def carry_right(cut):
+        return remote(
+            right1.at[cut], pass_b.at[cut],
+            near_sem.at[2, cut], near_sem.at[3, cut], (ka, other),
+        )
+
+    def to_last(cut):
+        return remote(
+            pass_a.at[cut], near.at[cut], near_sem.at[4, cut], near_sem.at[5, cut], (ka, other)
+        )
+
+    def to_first(cut):
+        return remote(
+            pass_b.at[cut], near.at[cut],
+            near_sem.at[6, cut], near_sem.at[5, cut], (at(1 - row), other),
+        )
+
+    def swap_wrap():
+        return remote(wrap_out, wrap_in, wrap_sem.at[0], wrap_sem.at[1], (ka, other))
 
     def swap_row():
         return remote(row_out, row_in, row_cross_sem.at[0], row_cross_sem.at[1], (ka, other))
@@ -163,15 +181,17 @@
         side = ga if same else other
         return remote(
             parts.at[job, side], inbox.at[slot],
-            result_sem.at[0, slot], result_sem.at[1, slot], (at(step * row), side),
+            result_sem.at[0, slot], result_sem.at[1, slot], (at(step), side),
         )
 
     RESULTS = (
         (ROW_JOB, 0, False), (NEXT_JOB, 0, False),
-        (PREV_JOB, -1, True), (PREV_JOB, -1, False),
-        (FAR_JOB, -2, True), (FAR_JOB, -2, False),
-        (BACK_JOB, 2, True), (BACK_JOB, 2, False),
+        (PREV_JOB, -row, True), (PREV_JOB, -row, False),
+        (FAR_JOB, -2 * row, True), (FAR_JOB, -2 * row, False),
+        (BACK_JOB, 2 * row, True), (BACK_JOB, 2 * row, False),
+        (WRAP_JOB, -1, True), (WRAP_JOB, -1, False),
     )
+    WRAPPED = (8, 9)
 
     def each(body):
         def run(c, carry):
@@ -210,25 +230,45 @@
             )
         return lax.fori_loop(0, count // STEP, run, total)
 
+    def packed_step(total, pairs):
+        left = jnp.concatenate([bra for bra, _ in pairs], axis=1)
+        right = jnp.concatenate(
+            [jnp.concatenate([ket for _, ket in pairs], axis=1),
+             jnp.concatenate([flipped(ket) for _, ket in pairs], axis=1)], axis=0
+        )
+        return total + lax.dot_general(
+            left, right, CONTRACT, preferred_element_type=jnp.float32
+        )
+
+    def packed_sums(totals, sources, count):
+        def run(s, totals):
+            return tuple(
+                packed_step(
+                    total, [(bra(s * STEP + u), ket(s * STEP + u)) for u in range(STEP)]
+                )
+                for total, (bra, ket) in zip(totals, sources)
+            )
+        return lax.fori_loop(0, count // STEP, run, tuple(totals))
+
     def packed_sum(total, bra, ket, count):
-        def run(s, total):
-            left = jnp.concatenate([bra(s * STEP + u) for u in range(STEP)], axis=1)
-            kets = [ket(s * STEP + u) for u in range(STEP)]
-            right = jnp.concatenate(
-                [jnp.concatenate(kets, axis=1),
-                 jnp.concatenate([flipped(k) for k in kets], axis=1)], axis=0
-            )
-            return total + lax.dot_general(
-                left, right, CONTRACT, preferred_element_type=jnp.float32
-            )
-        return lax.fori_loop(0, count // STEP, run, total)
+        return packed_sums((total,), ((bra, ket),), count)[0]
 
     def keep(job, total):
         parts[job] = total.reshape(parts.shape[1:])
 
     zero = jnp.zeros((bands, 2 * bands), jnp.float32)
 
+    small = [
+        pltpu.make_async_copy(given, held, small_sem.at[i])
+        for i, (given, held) in enumerate(
+            ((neighbour_in, neighbour), (shift_in, shift_id), (map_in, block_map))
+        )
+    ]
+    for copy in small:
+        copy.start()
     each(lambda c: load(c).start())
+    for copy in small:
+        copy.wait()
 
     tile = (8, lanes)
     columns = neighbour.shape[1]
@@ -245,44 +285,38 @@
     row_shift, next_shift, far_shift = [shift_of(step) for step in steps]
     shifts_out[0] = next_shift
     shifts_out[1] = far_shift
+    shifts_out[2] = row_shift
 
     def send_shift(i):
         return remote(
-            shifts_out.at[min(i, 1)], shifts_in.at[i],
-            shift_sem.at[0, i], shift_sem.at[1, i], (at((row, 2 * row, -2 * row)[i]), ga),
+            shifts_out.at[(0, 1, 1, 2)[i]], shifts_in.at[i],
+            shift_sem.at[0, i], shift_sem.at[1, i], (at((row, 2 * row, -2 * row, 1)[i]), ga),
         )
 
     barrier = pltpu.get_barrier_semaphore()
     meet = [
         (ka, other), (at(row), ga), (at(-row), ga), (at(row), other), (at(-row), other),
         (at(2 * row), ga), (at(-2 * row), ga), (at(2 * row), other), (at(-2 * row), other),
-        (at(-1), jnp.where(core == 1, ga, other)), (at(1), jnp.where(core == 0, ga, other)),
+        (at(-1), ga), (at(1), ga), (at(-1), other), (at(1), other),
         (at(aside), ga), (at(aside + row), ga), (at(aside - row), ga),
     ]
-    paths = row // 2
-
     def greet(device):
         pl.semaphore_signal(barrier, inc=1, device_id=device, device_id_type=MESH)
 
     for device in meet:
         greet(device)
 
-    @pl.when(place == 0)
-    def _():
-        for p in range(1, paths):
-            greet((at(2 * p), other))
-
-    @pl.when(place == row - 1)
-    def _():
-        for p in range(1, paths):
-            greet((at(1 + 2 * p), other))
-
-    between = (core == 0) & (place > 0)
-
-    @pl.when(between)
-    def _():
-        greet((at(-place), other))
-        greet((at(-1 - place), other))
+    @pl.when(first)
+    def _():
+        greet((at(row - 1), other))
+
+    @pl.when(last)
+    def _():
+        greet((at(1 - row), other))
+
+    def load_cut(cut):
+        load(2 * cut).wait()
+        load(2 * cut + 1).wait()
 
     def pack_cut(cut):
         def pack(t, carry):
@@ -296,13 +330,10 @@
             return carry
         lax.fori_loop(0, blocks // STEP, pack, 0)
 
-    each(lambda c: load(c).wait())
+    load_cut(0)
     pack_cut(0)
-    ends = (place == 0) | (place == row - 1)
-    pl.semaphore_wait(
-        barrier, len(meet) + jnp.where(ends, paths - 1, 0) + jnp.where(between, 2, 0)
-    )
-    for i in range(3):
+    pl.semaphore_wait(barrier, len(meet) + jnp.where(first | last, 1, 0))
+    for i in range(4):
         send_shift(i).start()
 
     def make_table():
@@ -316,7 +347,7 @@
             for a in range(2)
         ]
         maps = [jnp.where(ga == a, maps[0], maps[1]) for a in range(2)]
-        shifts = [row_shift, next_shift] + [shifts_in[i] for i in range(3)]
+        shifts = [row_shift, next_shift] + [shifts_in[i] for i in range(4)]
         choice = lax.broadcasted_iota(jnp.int32, tile, 0)
         rows = [
             jnp.sum(jnp.where(shift == choice, each_map, 0), axis=0, keepdims=True)
@@ -343,7 +374,7 @@
             jnp.sum(jnp.where(hits[r], local_t[:, r : r + 1], 0), axis=0, keepdims=True)
             for r in range(2 * JOBS)
         ]
-        lists += [jnp.zeros((1, lanes), jnp.int32)]
+        lists += [jnp.zeros((24 - 3 * JOBS, lanes), jnp.int32)]
         table_rows[...] = jnp.concatenate(lists, axis=0)
 
     def first_sends(c):
@@ -351,24 +382,22 @@
         def _():
             row_direct(c).start()
 
-        @pl.when((core == 0) & ((place > 0) | (c == 0)))
+        @pl.when((core == 0) & (place > 0))
         def _():
             row_relayed(c).start()
 
-        @pl.when((place == 0) & (c > 0))
-        def _():
-            to_via(c).start()
-
-    each(first_sends)
     hop_right(0).start()
     hop_left(0).start()
+    for cut in range(1, CUTS):
+        load_cut(cut)
+    each(first_sends)
     pack_cut(1)
     for cut in range(1, CUTS):
         if cut + 1 < CUTS:
             pack_cut(cut + 1)
         hop_right(cut).start()
         hop_left(cut).start()
-    for i in range(3):
+    for i in range(4):
         send_shift(i).wait_recv()
     make_table()
     fetch = pltpu.make_async_copy(table_rows, table, table_sem)
@@ -377,33 +406,56 @@
     gather(cross_out.at[0], lambda t: whole(packed.at[1 - next_half], bra_at(NEXT_JOB, inside + t)))
     gather(cross_out.at[1], lambda t: whole(packed.at[half], far_ket_at(PREV_JOB, t)))
 
+    @pl.when(core == 0)
+    def _():
+        gather(row_out, lambda t: own[bra_at(ROW_JOB, inside + t)])
+
+    @pl.when(last)
+    def _():
+        gather(
+            row_out,
+            lambda t: jnp.concatenate(
+                [whole(packed.at[h], bra_at(ROW_JOB, inside + t)) for h in range(2)], axis=0
+            ),
+        )
+
     @pl.when(needs_row)
     def _():
-        gather(row_out, lambda t: own[bra_at(ROW_JOB, inside + t)])
         swap_row().start()
+
+    @pl.when(first)
+    def _():
+        gather(wrap_out, lambda t: whole(packed.at[half], far_ket_at(WRAP_JOB, t)))
+        swap_wrap().start()
 
     swap(0).start()
     swap(1).start()
 
     @pl.when(quad == 3)
     def _():
-        for turn in RIGHT_BESIDE + RIGHT_OWN:
+        for turn in RIGHT_ASIDE + RIGHT_OWN:
             gather(
                 extra_out.at[turn],
                 lambda t: whole(packed.at[1 - half], bra_at(NEXT_JOB, turn * cross + t)),
             )
-        for turn in RIGHT_BESIDE:
+        for turn in RIGHT_ASIDE:
             extra_aside(turn).start()
 
     @pl.when(quad == 0)
     def _():
-        for turn in LEFT_BESIDE + LEFT_OWN:
+        for turn in LEFT_ASIDE + LEFT_OWN:
             gather(
                 extra_out.at[turn],
                 lambda t: whole(packed.at[half], ket_at(PREV_JOB, turn * cross + t)),
             )
-        for turn in LEFT_BESIDE:
+        for turn in LEFT_ASIDE:
             extra_aside(turn).start()
+
+    def pass_near(cut):
+        carry_left(cut).wait_recv()
+        to_last(cut).start()
+        carry_right(cut).wait_recv()
+        to_first(cut).start()
 
     def relay_on(c):
         row_relayed(c).wait_recv()
@@ -414,23 +466,23 @@
         on_right(cut).start()
         hop_left(cut).wait_recv()
 
-        @pl.when(between & ((place - 2) // 4 == cut))
-        def _():
-            to_via(0).wait_recv()
-            from_via().start()
-
         on_left(cut).start()
+
+        @pl.when(first)
+        def _(cut=cut):
+            carry_left(cut).start()
+
+        @pl.when(last)
+        def _(cut=cut):
+            carry_right(cut).start()
+            if cut:
+                pass_near(cut - 1)
 
         @pl.when((core == 1) & (place < row - 1))
         def _(cut=cut):
             for c in range(cut * CHUNKS // CUTS, (cut + 1) * CHUNKS // CUTS):
                 relay_on(c)
 
-        if cut == 1:
-            @pl.when(place == row - 1)
-            def _():
-                relay_on(0)
-
     @pl.when(quad == 3)
     def _():
         for turn in RIGHT_OWN:
@@ -443,15 +495,19 @@
 
     @pl.when(beside == 3)
     def _():
-        for turn in RIGHT_BESIDE:
+        for turn in RIGHT_ASIDE:
             extra_aside(turn).wait_recv()
             extra_back(turn).start()
 
     @pl.when(beside == 0)
     def _():
-        for turn in LEFT_BESIDE:
+        for turn in LEFT_ASIDE:
             extra_aside(turn).wait_recv()
             extra_back(turn).start()
+
+    @pl.when(last)
+    def _():
+        pass_near(CUTS - 1)
 
     swap(0).wait_recv()
     total = packed_sum(
@@ -496,14 +552,14 @@
             inside,
         )
 
-        @pl.when(needs_row)
+        @pl.when(core == 0)
         def _():
             swap_row().wait_recv()
             row_total[...] = whole_sum(
                 row_total[...], lambda t: row_in[t], lambda t: ahead[far_ket_at(ROW_JOB, t)], cross
             )
 
-        @pl.when(jnp.logical_not(needs_row))
+        @pl.when(core == 1)
         def _():
             row_total[...] = whole_sum(
                 row_total[...],
@@ -524,6 +580,46 @@
     def _():
         along_row()
 
+    def wrap_at_last():
+        for cut in range(CUTS):
+            to_last(cut).wait_recv()
+        swap_row().wait_recv()
+        lines = pl.ds(pl.multiple_of((1 - half) * bands, bands), bands)
+        total = packed_sum(
+            zero,
+            lambda t: whole(packed.at[1 - half], bra_at(ROW_JOB, t)),
+            lambda t: whole(near, ket_at(ROW_JOB, t)),
+            inside,
+        )
+        total = packed_sum(
+            total,
+            lambda t: row_in[t, lines, :],
+            lambda t: whole(near, far_ket_at(ROW_JOB, t)),
+            cross,
+        )
+        keep(ROW_JOB, total)
+        result(0).start()
+
+    def wrap_at_first():
+        for cut in range(CUTS):
+            to_last(cut).wait_recv()
+        swap_wrap().wait_recv()
+        total = packed_sum(
+            zero,
+            lambda t: whole(near, bra_at(WRAP_JOB, t)),
+            lambda t: whole(packed.at[half], ket_at(WRAP_JOB, t)),
+            inside,
+        )
+        total = packed_sum(
+            total,
+            lambda t: whole(near, bra_at(WRAP_JOB, inside + t)),
+            lambda t: wrap_in[t],
+            cross,
+        )
+        keep(WRAP_JOB, total)
+        for slot in WRAPPED:
+            result(slot).start()
+
     def far_swaps(cut):
         on_right(cut).wait_recv()
         gather(far_out.at[0, cut], lambda t: right2[cut][bra_at(FAR_JOB, inside + t)])
@@ -539,81 +635,106 @@
         result(3).start()
 
     for cut in range(1, CUTS):
+        if cut == CUTS - 1:
+            @pl.when((core == 1) & (place > 1) & (place < row - 1))
+            def _():
+                along_row()
+
+            @pl.when(last)
+            def _():
+                wrap_at_last()
+
+            @pl.when(first)
+            def _():
+                wrap_at_first()
+
         far_swaps(cut)
+
+    def previous_extra():
+        def source(turn):
+            if turn * cross < inside:
+                ket = lambda t: whole(packed.at[half], ket_at(PREV_JOB, turn * cross + t))
+            else:
+                ket = lambda t: cross_in[1, t]
+            return lambda t: extra[turn, t], ket
+
+        totals = (zero, zero)
+        for turns in zip(RIGHT_OWN, RIGHT_ASIDE):
+            for turn in turns:
+                hop_extra(turn).wait_recv()
+            totals = packed_sums(totals, [source(turn) for turn in turns], cross)
+        keep(PREV_JOB, totals[0] + totals[1])
+        result(2).start()
+        result(3).start()
 
     for cut in range(CUTS):
         on_left(cut).wait_recv()
-    far = packed_sum(
-        zero,
-        lambda t: whole_far(bra_at(FAR_JOB, t)),
-        lambda t: whole(left2, ket_at(FAR_JOB, t)),
+    far, back = packed_sums(
+        (zero, zero),
+        (
+            (lambda t: whole_far(bra_at(FAR_JOB, t)), lambda t: whole(left2, ket_at(FAR_JOB, t))),
+            (lambda t: whole(left2, bra_at(BACK_JOB, t)), lambda t: whole_far(ket_at(BACK_JOB, t))),
+        ),
         inside,
     )
-    back = packed_sum(
-        zero,
-        lambda t: whole(left2, bra_at(BACK_JOB, t)),
-        lambda t: whole_far(ket_at(BACK_JOB, t)),
-        inside,
-    )
-
-    @pl.when(core == 1)
+
+    @pl.when(place == 1)
     def _():
         along_row()
 
     for cut in range(CUTS):
         swap_far(0, cut).wait_recv()
         swap_far(1, cut).wait_recv()
-    far = packed_sum(
-        far,
-        lambda t: whole(far_in.at[0], t),
-        lambda t: whole(left2, far_ket_at(FAR_JOB, t)),
+    far, back = packed_sums(
+        (far, back),
+        (
+            (
+                lambda t: whole(far_in.at[0], t),
+                lambda t: whole(left2, far_ket_at(FAR_JOB, t)),
+            ),
+            (
+                lambda t: whole(left2, bra_at(BACK_JOB, inside + t)),
+                lambda t: whole(far_in.at[1], t),
+            ),
+        ),
         cross,
     )
     keep(FAR_JOB, far)
-    back = packed_sum(
-        back,
-        lambda t: whole(left2, bra_at(BACK_JOB, inside + t)),
-        lambda t: whole(far_in.at[1], t),
-        cross,
-    )
     keep(BACK_JOB, back)
     for slot in (4, 5, 6, 7):
         result(slot).start()
 
+    @pl.when(quad == 0)
+    def _():
+        previous_extra()
+
     @pl.when(quad == 3)
     def _():
-        more = zero
         for turn in LEFT:
             hop_extra(turn).wait_recv()
-            more = packed_sum(
-                more,
+
+        def source(turn):
+            return (
                 lambda t: whole(packed.at[1 - half], bra_at(NEXT_JOB, turn * cross + t)),
                 lambda t: extra[turn, t],
-                cross,
             )
-        keep(NEXT_JOB, parts[NEXT_JOB].reshape(zero.shape) + more)
+
+        more = packed_sums((zero, zero), [source(turn) for turn in LEFT], cross)
+        keep(NEXT_JOB, parts[NEXT_JOB].reshape(zero.shape) + (more[0] + more[1]))
         result(1).start()
 
-    @pl.when(quad == 0)
-    def _():
-        total = zero
-        for turn in RIGHT:
-            hop_extra(turn).wait_recv()
-            total = packed_sum(
-                total,
-                lambda t: extra[turn, t],
-                (lambda t: whole(packed.at[half], ket_at(PREV_JOB, turn * cross + t)))
-                if turn * cross < inside else (lambda t: cross_in[1, t]),
-                cross,
-            )
-        keep(PREV_JOB, total)
-        result(2).start()
-        result(3).start()
-
-    for slot in range(len(RESULTS)):
+    for slot in range(WRAPPED[0]):
         result(slot).wait_recv()
+    inbox[0] = inbox[0] + parts[ROW_JOB, ga]
+
+    @pl.when(last)
+    def _():
+        for slot in WRAPPED:
+            result(slot).wait_recv()
+        inbox[0] = inbox[0] + (inbox[8] + inbox[9])
+
     found = [
-        parts[ROW_JOB, ga] + inbox[0],
+        inbox[0],
         (parts[NEXT_JOB, ga] + inbox[1]) + (inbox[2] + inbox[3]),
         (inbox[4] + inbox[5]) + (inbox[6] + inbox[7]),
     ]
@@ -626,9 +747,11 @@
         out[b, 1] = chosen[:, bands:]
 
     def drain(c):
-        row_direct(c).wait_send()
-
-        @pl.when((core == 1) & ((place < row - 1) | (c == 0)))
+        @pl.when(place > 0)
+        def _():
+            row_direct(c).wait_send()
+
+        @pl.when((core == 1) & (place < row - 1))
         def _():
             relayed(c).wait_send()
 
@@ -640,7 +763,7 @@
         on_left(cut).wait_send()
         swap_far(0, cut).wait_send()
         swap_far(1, cut).wait_send()
-    for i in range(3):
+    for i in range(4):
         send_shift(i).wait_send()
 
     @pl.when(quad == 3)
@@ -655,18 +778,28 @@
 
     @pl.when(beside == 3)
     def _():
-        for turn in RIGHT_BESIDE:
+        for turn in RIGHT_ASIDE:
             extra_back(turn).wait_send()
 
     @pl.when(beside == 0)
     def _():
-        for turn in LEFT_BESIDE:
+        for turn in LEFT_ASIDE:
             extra_back(turn).wait_send()
 
-    @pl.when(between)
-    def _():
-        from_via().wait_send()
-
+    @pl.when(first)
+    def _():
+        swap_wrap().wait_send()
+        for cut in range(CUTS):
+            carry_left(cut).wait_send()
+        for slot in WRAPPED:
+            result(slot).wait_send()
+
+    @pl.when(last)
+    def _():
+        for cut in range(CUTS):
+            carry_right(cut).wait_send()
+            to_last(cut).wait_send()
+            to_first(cut).wait_send()
 
     @pl.when(needs_row)
     def _():
@@ -674,7 +807,7 @@
 
     for i in range(2):
         swap(i).wait_send()
-    for slot in range(len(RESULTS)):
+    for slot in range(WRAPPED[0]):
         result(slot).wait_send()
 
 
@@ -697,40 +830,47 @@
         functools.partial(kernel, n_ka, row, cross),
         out_shape=jax.ShapeDtypeStruct((columns, 2, bands // 2, bands), jnp.float32),
         in_specs=[
-            pl.BlockSpec(memory_space=pltpu.VMEM),
-            pl.BlockSpec(memory_space=pltpu.VMEM),
-            pl.BlockSpec(memory_space=pltpu.VMEM),
+            pl.BlockSpec(memory_space=pl.ANY),
+            pl.BlockSpec(memory_space=pl.ANY),
+            pl.BlockSpec(memory_space=pl.ANY),
             pl.BlockSpec(memory_space=pl.ANY),
         ],
         out_specs=pl.BlockSpec(memory_space=pltpu.VMEM),
         scratch_shapes=[
-            pltpu.VMEM((2, 8, lanes), jnp.int32),
+            pltpu.VMEM(neighbour.shape, jnp.int32),
+            pltpu.VMEM(shift_id.shape, jnp.int32),
+            pltpu.VMEM(block_map.shape, jnp.int32),
             pltpu.VMEM((3, 8, lanes), jnp.int32),
-            pltpu.VMEM((16, lanes), jnp.int32),
-            pltpu.SMEM((16, lanes), jnp.int32),
+            pltpu.VMEM((4, 8, lanes), jnp.int32),
+            pltpu.VMEM((24, lanes), jnp.int32),
+            pltpu.SMEM((24, lanes), jnp.int32),
             whole_buffer(blocks),
             cut_buffer(2, CUTS, blocks),
             cut_buffer(CUTS, blocks),
             *[cut_buffer(blocks) for _ in range(CUTS)],
             cut_buffer(CUTS, blocks), cut_buffer(CUTS, blocks),
             half_buffer(TURNS, cross), half_buffer(TURNS, cross), half_buffer(TURNS, cross),
-            whole_buffer(blocks), whole_buffer(blocks // CHUNKS), whole_buffer(blocks),
+            whole_buffer(blocks), whole_buffer(blocks),
+            cut_buffer(CUTS, blocks), cut_buffer(CUTS, blocks), cut_buffer(CUTS, blocks),
+            half_buffer(cross), half_buffer(cross),
             whole_buffer(cross), whole_buffer(cross),
             half_buffer(2, cross), half_buffer(2, cross),
             cut_buffer(2, CUTS, cross), cut_buffer(2, CUTS, cross),
             pltpu.VMEM((2 * bands, 2 * bands), jnp.float32),
-            pltpu.VMEM((5, 2, bands // 2, 2 * bands), jnp.float32),
-            pltpu.VMEM((8, bands // 2, 2 * bands), jnp.float32),
+            pltpu.VMEM((JOBS, 2, bands // 2, 2 * bands), jnp.float32),
+            pltpu.VMEM((10, bands // 2, 2 * bands), jnp.float32),
+            pltpu.SemaphoreType.DMA((3,)),
             pltpu.SemaphoreType.DMA((5, CHUNKS)),
             pltpu.SemaphoreType.DMA((8, CUTS)),
-            pltpu.SemaphoreType.DMA((2, 3)),
+            pltpu.SemaphoreType.DMA((2, 4)),
             pltpu.SemaphoreType.DMA,
+            pltpu.SemaphoreType.DMA((7, CUTS)),
             pltpu.SemaphoreType.DMA((2,)),
             pltpu.SemaphoreType.DMA((4, TURNS)),
             pltpu.SemaphoreType.DMA((2,)),
             pltpu.SemaphoreType.DMA((2, 2)),
             pltpu.SemaphoreType.DMA((2, 2, CUTS)),
-            pltpu.SemaphoreType.DMA((2, 8)),
+            pltpu.SemaphoreType.DMA((2, 10)),
         ],
         compiler_params=pltpu.CompilerParams(
             collective_id=0, has_side_effects=True, vmem_limit_bytes=61 * 2**20

time: 117 us -> 110 us (0.940); the launches traced: 114 us -> 110 us
  Pallas kernels: 113 us -> 109 us
    pallas_call x1, Pallas kernels: 113 us -> 109 us  [on_device(): pl.pallas_call(functools.partial(kernel, n_ka, row, cross), out_shape=jax...]
where the time goes in v5:
time: 110 us
  Pallas kernels  109 us (99%)
  local copies, waits for them, and re-layouts  1.54 us (1%)
    pallas_call x1, Pallas kernels, on_device(): pl.pallas_call(functools.partial(kernel, n_ka, row, cross), out_shape=jax...  109 us

profile of v5, /device:TPU:2, one launch (start us, length us, event | category | flops | bytes accessed | tf_op | source)
XLA Modules:
  0.0 110.2 jit_solution(7867143612609743636)
XLA Ops:
  0.0 108.6 %overlaps.1 = f32[3,2,32,64]{3,2,1,0:T(8,128)} custom-call(s32[1,3]{1,0:T(1,128)} %neighbour_in.1, s32[1,3]{1,0:T(1,128)} %shift_in.1, s32[8,240]{1,0:T(8,128)} %map_in.1, bf16[120,128,128]{2,1,0:T(8,128)(2,1)} %bitcast.2), custom_call_target="tpu_custom_call" | custom-call | tf_op jit(solution)/shard_map/overlaps/pallas_call | solution.py:829
  108.6 1.5 %copy.6 = f32[1,3,2,32,64]{4,3,2,1,0:T(8,128)} copy(f32[1,3,2,32,64]{4,3,2,1,0:T(8,128)} %bitcast.3) | data formatting | bytes 98304

commit v6 on v5

--- a/solution.py
+++ b/solution.py
@@ -10,9 +10,9 @@
 MESH = pl.DeviceIdType.MESH
 CHUNKS = 8
 CUTS = 4
-TURNS = 6
-LEFT_OWN, LEFT_ASIDE = (0,), (1,)
-RIGHT_OWN, RIGHT_ASIDE = (2, 3), (4, 5)
+TURNS = 12
+LEFT_OWN, LEFT_ASIDE = (0, 1, 2), (3, 4, 5)
+RIGHT_OWN, RIGHT_ASIDE = (6, 7, 8), (9, 10, 11)
 LEFT = LEFT_OWN + LEFT_ASIDE
 RIGHT = RIGHT_OWN + RIGHT_ASIDE
 PACK = 5
@@ -46,6 +46,7 @@
     right2 = (right2_0, right2_1, right2_2, right2_3)
     size = blocks // CHUNKS
     inside = blocks - cross
+    turn_size = blocks // TURNS
     ka = lax.axis_index("ka")
     ga = lax.axis_index("ga")
     other = 1 - ga
@@ -214,12 +215,12 @@
     def whole_far(index):
         return jnp.concatenate([right2[cut][index] for cut in range(CUTS)], axis=0)
 
-    def gather(target, pick):
+    def gather(target, pick, count=cross):
         def run(t, carry):
             for u in range(PACK):
                 target[t * PACK + u] = pick(t * PACK + u)
             return carry
-        lax.fori_loop(0, cross // PACK, run, 0)
+        lax.fori_loop(0, count // PACK, run, 0)
 
     def whole_sum(total, bra, ket, count):
         def run(s, total):
@@ -240,15 +241,15 @@
             left, right, CONTRACT, preferred_element_type=jnp.float32
         )
 
-    def packed_sums(totals, sources, count):
+    def packed_sums(totals, sources, count, width=STEP):
         def run(s, totals):
             return tuple(
                 packed_step(
-                    total, [(bra(s * STEP + u), ket(s * STEP + u)) for u in range(STEP)]
+                    total, [(bra(s * width + u), ket(s * width + u)) for u in range(width)]
                 )
                 for total, (bra, ket) in zip(totals, sources)
             )
-        return lax.fori_loop(0, count // STEP, run, tuple(totals))
+        return lax.fori_loop(0, count // width, run, tuple(totals))
 
     def packed_sum(total, bra, ket, count):
         return packed_sums((total,), ((bra, ket),), count)[0]
@@ -257,41 +258,6 @@
         parts[job] = total.reshape(parts.shape[1:])
 
     zero = jnp.zeros((bands, 2 * bands), jnp.float32)
-
-    small = [
-        pltpu.make_async_copy(given, held, small_sem.at[i])
-        for i, (given, held) in enumerate(
-            ((neighbour_in, neighbour), (shift_in, shift_id), (map_in, block_map))
-        )
-    ]
-    for copy in small:
-        copy.start()
-    each(lambda c: load(c).start())
-    for copy in small:
-        copy.wait()
-
-    tile = (8, lanes)
-    columns = neighbour.shape[1]
-    targets = [jnp.broadcast_to(neighbour[:, b : b + 1], tile) for b in range(columns)]
-    steps = (1, row, n_ka // 2)
-
-    def shift_of(step):
-        found = jnp.zeros(tile, jnp.int32)
-        for b in range(columns):
-            moved = jnp.broadcast_to(shift_id[:, b : b + 1], tile)
-            found = found + jnp.where(targets[b] == at(step), moved, 0)
-        return found
-
-    row_shift, next_shift, far_shift = [shift_of(step) for step in steps]
-    shifts_out[0] = next_shift
-    shifts_out[1] = far_shift
-    shifts_out[2] = row_shift
-
-    def send_shift(i):
-        return remote(
-            shifts_out.at[(0, 1, 1, 2)[i]], shifts_in.at[i],
-            shift_sem.at[0, i], shift_sem.at[1, i], (at((row, 2 * row, -2 * row, 1)[i]), ga),
-        )
 
     barrier = pltpu.get_barrier_semaphore()
     meet = [
@@ -313,6 +279,41 @@
     @pl.when(last)
     def _():
         greet((at(1 - row), other))
+
+    small = [
+        pltpu.make_async_copy(given, held, small_sem.at[i])
+        for i, (given, held) in enumerate(
+            ((neighbour_in, neighbour), (shift_in, shift_id), (map_in, block_map))
+        )
+    ]
+    for copy in small:
+        copy.start()
+    each(lambda c: load(c).start())
+    for copy in small:
+        copy.wait()
+
+    tile = (8, lanes)
+    columns = neighbour.shape[1]
+    targets = [jnp.broadcast_to(neighbour[:, b : b + 1], tile) for b in range(columns)]
+    steps = (1, row, n_ka // 2)
+
+    def shift_of(step):
+        found = jnp.zeros(tile, jnp.int32)
+        for b in range(columns):
+            moved = jnp.broadcast_to(shift_id[:, b : b + 1], tile)
+            found = found + jnp.where(targets[b] == at(step), moved, 0)
+        return found
+
+    row_shift, next_shift, far_shift = [shift_of(step) for step in steps]
+    shifts_out[0] = next_shift
+    shifts_out[1] = far_shift
+    shifts_out[2] = row_shift
+
+    def send_shift(i):
+        return remote(
+            shifts_out.at[(0, 1, 1, 2)[i]], shifts_in.at[i],
+            shift_sem.at[0, i], shift_sem.at[1, i], (at((row, 2 * row, -2 * row, 1)[i]), ga),
+        )
 
     def load_cut(cut):
         load(2 * cut).wait()
@@ -436,7 +437,8 @@
         for turn in RIGHT_ASIDE + RIGHT_OWN:
             gather(
                 extra_out.at[turn],
-                lambda t: whole(packed.at[1 - half], bra_at(NEXT_JOB, turn * cross + t)),
+                lambda t: whole(packed.at[1 - half], bra_at(NEXT_JOB, turn * turn_size + t)),
+                turn_size,
             )
         for turn in RIGHT_ASIDE:
             extra_aside(turn).start()
@@ -446,7 +448,8 @@
         for turn in LEFT_ASIDE + LEFT_OWN:
             gather(
                 extra_out.at[turn],
-                lambda t: whole(packed.at[half], ket_at(PREV_JOB, turn * cross + t)),
+                lambda t: whole(packed.at[half], ket_at(PREV_JOB, turn * turn_size + t)),
+                turn_size,
             )
         for turn in LEFT_ASIDE:
             extra_aside(turn).start()
@@ -636,7 +639,7 @@
 
     for cut in range(1, CUTS):
         if cut == CUTS - 1:
-            @pl.when((core == 1) & (place > 1) & (place < row - 1))
+            @pl.when((core == 1) & (place < row - 1))
             def _():
                 along_row()
 
@@ -650,22 +653,32 @@
 
         far_swaps(cut)
 
-    def previous_extra():
-        def source(turn):
-            if turn * cross < inside:
-                ket = lambda t: whole(packed.at[half], ket_at(PREV_JOB, turn * cross + t))
-            else:
-                ket = lambda t: cross_in[1, t]
-            return lambda t: extra[turn, t], ket
-
+    def previous_extra(turn):
+        if turn * turn_size < inside:
+            ket = lambda t: whole(packed.at[half], ket_at(PREV_JOB, turn * turn_size + t))
+        else:
+            ket = lambda t: cross_in[1, turn * turn_size - inside + t]
+        return lambda t: extra[turn, t], ket
+
+    def next_extra(turn):
+        return (
+            lambda t: whole(packed.at[1 - half], bra_at(NEXT_JOB, turn * turn_size + t)),
+            lambda t: extra[turn, t],
+        )
+
+    def extra_sum(turns, source):
         totals = (zero, zero)
-        for turns in zip(RIGHT_OWN, RIGHT_ASIDE):
-            for turn in turns:
+        for pair in turns:
+            for turn in pair:
                 hop_extra(turn).wait_recv()
-            totals = packed_sums(totals, [source(turn) for turn in turns], cross)
-        keep(PREV_JOB, totals[0] + totals[1])
-        result(2).start()
-        result(3).start()
+            totals = packed_sums(totals, [source(turn) for turn in pair], turn_size, turn_size)
+        return totals[0] + totals[1]
+
+    def kept(job):
+        return parts[job].reshape(zero.shape)
+
+    from_left = tuple(zip(RIGHT_OWN, RIGHT_ASIDE))
+    from_right = tuple(zip(LEFT_OWN, LEFT_ASIDE))
 
     for cut in range(CUTS):
         on_left(cut).wait_recv()
@@ -678,9 +691,13 @@
         inside,
     )
 
-    @pl.when(place == 1)
-    def _():
-        along_row()
+    @pl.when(quad == 0)
+    def _():
+        keep(PREV_JOB, extra_sum(from_left[:2], previous_extra))
+
+    @pl.when(quad == 3)
+    def _():
+        keep(NEXT_JOB, kept(NEXT_JOB) + extra_sum(from_right[:2], next_extra))
 
     for cut in range(CUTS):
         swap_far(0, cut).wait_recv()
@@ -706,45 +723,14 @@
 
     @pl.when(quad == 0)
     def _():
-        previous_extra()
+        keep(PREV_JOB, kept(PREV_JOB) + extra_sum(from_left[2:], previous_extra))
+        result(2).start()
+        result(3).start()
 
     @pl.when(quad == 3)
     def _():
-        for turn in LEFT:
-            hop_extra(turn).wait_recv()
-
-        def source(turn):
-            return (
-                lambda t: whole(packed.at[1 - half], bra_at(NEXT_JOB, turn * cross + t)),
-                lambda t: extra[turn, t],
-            )
-
-        more = packed_sums((zero, zero), [source(turn) for turn in LEFT], cross)
-        keep(NEXT_JOB, parts[NEXT_JOB].reshape(zero.shape) + (more[0] + more[1]))
+        keep(NEXT_JOB, kept(NEXT_JOB) + extra_sum(from_right[2:], next_extra))
         result(1).start()
-
-    for slot in range(WRAPPED[0]):
-        result(slot).wait_recv()
-    inbox[0] = inbox[0] + parts[ROW_JOB, ga]
-
-    @pl.when(last)
-    def _():
-        for slot in WRAPPED:
-            result(slot).wait_recv()
-        inbox[0] = inbox[0] + (inbox[8] + inbox[9])
-
-    found = [
-        inbox[0],
-        (parts[NEXT_JOB, ga] + inbox[1]) + (inbox[2] + inbox[3]),
-        (inbox[4] + inbox[5]) + (inbox[6] + inbox[7]),
-    ]
-    for b in range(columns):
-        target = jnp.broadcast_to(neighbour[:, b : b + 1], found[0].shape)
-        chosen = jnp.where(
-            target == at(steps[0]), found[0], jnp.where(target == at(steps[1]), found[1], found[2])
-        )
-        out[b, 0] = chosen[:, :bands]
-        out[b, 1] = chosen[:, bands:]
 
     def drain(c):
         @pl.when(place > 0)
@@ -791,8 +777,6 @@
         swap_wrap().wait_send()
         for cut in range(CUTS):
             carry_left(cut).wait_send()
-        for slot in WRAPPED:
-            result(slot).wait_send()
 
     @pl.when(last)
     def _():
@@ -808,7 +792,35 @@
     for i in range(2):
         swap(i).wait_send()
     for slot in range(WRAPPED[0]):
+        result(slot).wait_recv()
+    inbox[0] = inbox[0] + parts[ROW_JOB, ga]
+
+    @pl.when(last)
+    def _():
+        for slot in WRAPPED:
+            result(slot).wait_recv()
+        inbox[0] = inbox[0] + (inbox[8] + inbox[9])
+
+    found = [
+        inbox[0],
+        (parts[NEXT_JOB, ga] + inbox[1]) + (inbox[2] + inbox[3]),
+        (inbox[4] + inbox[5]) + (inbox[6] + inbox[7]),
+    ]
+    for b in range(columns):
+        target = jnp.broadcast_to(neighbour[:, b : b + 1], found[0].shape)
+        chosen = jnp.where(
+            target == at(steps[0]), found[0], jnp.where(target == at(steps[1]), found[1], found[2])
+        )
+        out[b, 0] = chosen[:, :bands]
+        out[b, 1] = chosen[:, bands:]
+
+    for slot in range(WRAPPED[0]):
         result(slot).wait_send()
+
+    @pl.when(first)
+    def _():
+        for slot in WRAPPED:
+            result(slot).wait_send()
 
 
 def on_device(coeffs, neighbour, shift_id, block_map):
@@ -828,7 +840,7 @@
 
     found = pl.pallas_call(
         functools.partial(kernel, n_ka, row, cross),
-        out_shape=jax.ShapeDtypeStruct((columns, 2, bands // 2, bands), jnp.float32),
+        out_shape=pltpu.VMEM((columns, 2, bands // 2, bands), jnp.float32),
         in_specs=[
             pl.BlockSpec(memory_space=pl.ANY),
             pl.BlockSpec(memory_space=pl.ANY),
@@ -849,7 +861,7 @@
             cut_buffer(CUTS, blocks),
             *[cut_buffer(blocks) for _ in range(CUTS)],
             cut_buffer(CUTS, blocks), cut_buffer(CUTS, blocks),
-            half_buffer(TURNS, cross), half_buffer(TURNS, cross), half_buffer(TURNS, cross),
+            *[half_buffer(TURNS, blocks // TURNS) for _ in range(3)],
             whole_buffer(blocks), whole_buffer(blocks),
             cut_buffer(CUTS, blocks), cut_buffer(CUTS, blocks), cut_buffer(CUTS, blocks),
             half_buffer(cross), half_buffer(cross),

time: 110 us -> 108 us (0.982)
  no operation moved by 1% of the time
where the time goes in v6:
time: 108 us
  Pallas kernels  108 us (100%)
    pallas_call x1, Pallas kernels, on_device(): pl.pallas_call(functools.partial(kernel, n_ka, row, cross), out_shape=plt...  108 us

profile of v6, /device:TPU:2, one launch (start us, length us, event | category | flops | bytes accessed | tf_op | source)
XLA Modules:
  0.0 108.3 jit_solution(820520209681121178)
XLA Ops:
  0.0 107.7 %overlaps.1 = f32[3,2,32,64]{3,2,1,0:T(8,128)S(1)} custom-call(s32[1,3]{1,0:T(1,128)} %neighbour_in.1, s32[1,3]{1,0:T(1,128)} %shift_in.1, s32[8,240]{1,0:T(8,128)} %map_in.1, bf16[120,128,128]{2,1,0:T(8,128)(2,1)} %bitcast.3), custom_call_target="tpu_custom_call" | custom-call | tf_op jit(solution)/shard_map/overlaps/pallas_call | solution.py:841
  107.7 0.6 copy.6

commit v7 on v6

--- a/solution.py
+++ b/solution.py
@@ -288,7 +288,8 @@
     ]
     for copy in small:
         copy.start()
-    each(lambda c: load(c).start())
+    load(0).start()
+    load(1).start()
     for copy in small:
         copy.wait()
 
@@ -332,6 +333,8 @@
         lax.fori_loop(0, blocks // STEP, pack, 0)
 
     load_cut(0)
+    for i in range(2, CHUNKS):
+        load(i).start()
     pack_cut(0)
     pl.semaphore_wait(barrier, len(meet) + jnp.where(first | last, 1, 0))
     for i in range(4):

time: 108 us -> 108 us (level)
  no operation moved by 1% of the time
where the time goes in v7:
time: 108 us
  Pallas kernels  108 us (100%)
    pallas_call x1, Pallas kernels, on_device(): pl.pallas_call(functools.partial(kernel, n_ka, row, cross), out_shape=plt...  108 us

profile of v7, /device:TPU:2, one launch (start us, length us, event | category | flops | bytes accessed | tf_op | source)
XLA Modules:
  0.0 108.3 jit_solution(3277383299822014088)
XLA Ops:
  0.0 107.7 %overlaps.1 = f32[3,2,32,64]{3,2,1,0:T(8,128)S(1)} custom-call(s32[1,3]{1,0:T(1,128)} %neighbour_in.1, s32[1,3]{1,0:T(1,128)} %shift_in.1, s32[8,240]{1,0:T(8,128)} %map_in.1, bf16[120,128,128]{2,1,0:T(8,128)(2,1)} %bitcast.3), custom_call_target="tpu_custom_call" | custom-call | tf_op jit(solution)/shard_map/overlaps/pallas_call | solution.py:844
  107.7 0.6 copy.6
